TPU v7x, 256 devices: a whole 4x4x8 slice. The times are simulated.
256 devices in a mesh: rep: 1, r: 32 (over y, z), s: 8 (over x, core).
Axes of the slice: x: 4, y: 4, z: 8, core: 2. Of those that a mesh axis runs over, the one named last changes fastest.
Arguments:
- x: bfloat16 [256, 2048, 1024], P(('rep', 'r', 's'))
- dy: bfloat16 [256, 2048, 1024], P(('rep', 'r', 's'))
- w_gate: bfloat16 [2, 1024, 3200], P(None, 's')
- w_up: bfloat16 [2, 1024, 3200], P(None, 's')
- w_down: bfloat16 [2, 3200, 1024], P(None, 's')
- m_w_gate: float32 [2, 1024, 3200], P(None, 's')
- m_w_up: float32 [2, 1024, 3200], P(None, 's')
- m_w_down: float32 [2, 3200, 1024], P(None, 's')
- v_w_gate: float32 [2, 1024, 3200], P(None, 's')
- v_w_up: float32 [2, 1024, 3200], P(None, 's')
- v_w_down: float32 [2, 3200, 1024], P(None, 's')
Outputs:
- output 1: bfloat16 [2, 1024, 3200], P('rep', 's')
- output 2: bfloat16 [2, 1024, 3200], P('rep', 's')
- output 3: bfloat16 [2, 3200, 1024], P('rep', 's')
- output 4: float32 [2, 1024, 3200], P('rep', 's')
- output 5: float32 [2, 1024, 3200], P('rep', 's')
- output 6: float32 [2, 3200, 1024], P('rep', 's')
- output 7: float32 [2, 1024, 3200], P('rep', 's')
- output 8: float32 [2, 1024, 3200], P('rep', 's')
- output 9: float32 [2, 3200, 1024], P('rep', 's')
All inputs are finite; a program needn't handle non-finite values.
Results may differ from a plain program's by a relative error of at most 0.022.
Values are sent between devices in bfloat16 or wider.
A program may use at most 768 MiB of HBM per device.

v0:
```python
import jax
import jax.numpy as jnp
from jax import lax
from jax.sharding import PartitionSpec as P

NAMES = ("w_gate", "w_up", "w_down")


def matmul(a, w):
    return jnp.dot(a, w, preferred_element_type=jnp.float32).astype(jnp.bfloat16)


def normed(h):
    wide = h.astype(jnp.float32)
    scale = lax.rsqrt(jnp.mean(wide**2, -1, keepdims=True) + 1e-6)
    return (wide * scale).astype(jnp.bfloat16)


def layer(h, w):
    a = normed(h)
    gate = jnp.dot(a, w["w_gate"], preferred_element_type=jnp.float32)
    up = jnp.dot(a, w["w_up"], preferred_element_type=jnp.float32)
    return h + matmul((jax.nn.silu(gate) * up).astype(jnp.bfloat16), w["w_down"])


def adamw(w, m, v, g):
    m = 0.9 * m + 0.1 * g
    v = 0.95 * v + 0.05 * g * g
    step = m * lax.rsqrt(v + 1e-8) + 0.1 * w
    return (w - 0.02 * step).astype(jnp.bfloat16), m, v


def solution(mesh):
    def fetched(weights, number):
        return {name: lax.all_gather(w[number], "s", axis=0, tiled=True) for name, w in zip(NAMES, weights, strict=True)}

    def summed(term):
        return lax.psum(lax.psum_scatter(term, "s", scatter_dimension=0, tiled=True), "r")

    def step(x, dy, *arrays):
        weights, m, v = (arrays[i : i + 3] for i in (0, 3, 6))
        layers = weights[0].shape[0]
        h, kept = x[0], []
        for number in range(layers):
            kept.append(h)
            h = layer(h, fetched(weights, number))
        by_h, mine = dy[0], [None] * layers
        for number in reversed(range(layers)):
            _, back = jax.vjp(lambda w, h: layer(h, w), fetched(weights, number), kept[number])
            by_w, by_h = back(by_h)
            mine[number] = [summed(by_w[name]) for name in NAMES]
        gradients = [jnp.stack([mine[number][i] for number in range(layers)]).astype(jnp.float32) for i in range(3)]
        new = [adamw(w.astype(jnp.float32), m, v, g) for w, m, v, g in zip(weights, m, v, gradients, strict=True)]
        return tuple(one[which] for which in range(3) for one in new)

    states, cut = P(("rep", "r", "s"), None, None), P(None, "s", None)
    return jax.shard_map(
        step,
        mesh=mesh,
        in_specs=(states, states) + (cut,) * 9,
        out_specs=(P("rep", "s", None),) * 9,
        check_vma=False,
    )
```

profile of v0, /device:TPU:2, one launch (start us, length us, event | category | flops | bytes accessed | tf_op | source)
XLA Modules:
  0.0 891.2 jit_solution(2595995306733939512)
XLA Ops:
  7.2 0.0 all-gather.13.cloned.1.call-start
  7.2 2.8 fusion.88
  10.0 0.0 all-gather.13.cloned.1.call-update
  10.0 0.0 all-gather.15.cloned.1.call-start
  10.1 2.7 fusion.87
  12.8 0.0 all-gather.15.cloned.1.call-update
  12.8 0.0 all-gather.17.cloned.1.call-start
  12.8 1.3 fusion.86
  14.2 0.0 all-gather.21.cloned.1.call-start
  14.2 0.5 all-gather.21.cloned.1.call-update
  14.7 0.0 all-gather.23.cloned.1.call-start
  14.8 0.5 all-gather.23.cloned.1.call-update
  15.3 0.0 all-gather.19.cloned.1.call-start
  15.4 0.5 all-gather.19.cloned.1.call-update
  15.9 0.0 reduce-scatter.15.cloned.1.call-start
  15.9 6.5 copy.20
  22.5 3.1 fusion.15
  25.6 6.5 copy.21
  32.1 24.7 %all-gather.13.cloned.1.call-done = bf16[1,1024,3200]{2,1,0:T(8,128)(2,1)} async-done(((bf16[1,128,3200]{2,1,0:T(8,128)(2,1)}), bf16[1,1024,3200]{2,1,0:T(8,128)(2,1)}) %all-gather.13.cloned.1.call-update) | async-done | bytes 6553616 | tf_op jit(solution)/shard_map/all_gather | solution.py:35
  56.8 22.9 %fusion.41 = f32[2048,3200]{1,0:T(8,128)} fusion(bf16[1,1024,3200]{2,1,0:T(8,128)(2,1)} %all-gather.13.cloned.1.call-done, bf16[1,2048,1024]{1,2,0:T(8,128)(2,1)} %copy.20, f32[2048]{0:T(1024)S(1)} %add_rsqrt_fusion), kind=kOutput, calls=%fused_computation.59 | convolution fusion | flops 13428064256 | bytes 36970496 | tf_op jit(solution)/shard_map/dot_general | solution.py:21
  79.7 24.0 %all-gather.15.cloned.1.call-done = bf16[1,1024,3200]{2,1,0:T(8,128)(2,1)} async-done(((bf16[1,128,3200]{2,1,0:T(8,128)(2,1)}), bf16[1,1024,3200]{2,1,0:T(8,128)(2,1)}) %all-gather.15.cloned.1.call-update) | async-done | bytes 6553616 | tf_op jit(solution)/shard_map/all_gather | solution.py:35
  103.7 31.4 %multiply_convert_fusion.1 = (bf16[2048,3200]{1,0:T(8,128)(2,1)}, f32[2048,3200]{1,0:T(8,128)}) fusion(f32[2048,3200]{1,0:T(8,128)} %fusion.41, bf16[1,1024,3200]{2,1,0:T(8,128)(2,1)} %all-gather.15.cloned.1.call-done, bf16[1,2048,1024]{1,2,0:T(8,128)(2,1)} %copy.20, f32[2048]{0:T(1024)S(1)} %add_rsqrt_fusion), kind=kOutput, calls=%fused_computation.17 | convolution fusion | flops 13467385856 | bytes 76292096 | tf_op jit(solution)/shard_map/dot_general | solution.py:22
  135.1 15.5 %all-gather.17.cloned.1.call-done = bf16[1,3200,1024]{2,1,0:T(8,128)(2,1)} async-done(((bf16[1,400,1024]{2,1,0:T(8,128)(2,1)}), bf16[1,3200,1024]{2,1,0:T(8,128)(2,1)}) %all-gather.17.cloned.1.call-update) | async-done | bytes 6553616 | tf_op jit(solution)/shard_map/all_gather | solution.py:35
  150.6 21.9 %fusion.19 = (f32[2048]{0:T(1024)S(1)}, bf16[2048,1024]{0,1:T(8,128)(2,1)}) fusion(bf16[2048,3200]{1,0:T(8,128)(2,1)} %get-tuple-element.30, bf16[1,3200,1024]{2,1,0:T(8,128)(2,1)} %all-gather.17.cloned.1.call-done, bf16[1,2048,1024]{1,2,0:T(8,128)(2,1)} %copy.20), kind=kOutput, calls=%fused_computation.37 | convolution fusion | flops 13432256512 | bytes 28057600 | tf_op jit(solution)/shard_map/dot_general | solution.py:10
  172.5 24.8 %all-gather.21.cloned.1.call-done = bf16[1,3200,1024]{2,1,0:T(8,128)(2,1)} async-done(((bf16[1,400,1024]{2,1,0:T(8,128)(2,1)}), bf16[1,3200,1024]{2,1,0:T(8,128)(2,1)}) %all-gather.21.cloned.1.call-update) | async-done | bytes 6553616 | tf_op jit(solution)/shard_map/all_gather | solution.py:35
  197.3 20.9 %convolution_convert_fusion.1 = bf16[2048,3200]{1,0:T(8,128)(2,1)} fusion(bf16[1,3200,1024]{2,1,0:T(8,128)(2,1)} %all-gather.21.cloned.1.call-done, bf16[1,2048,1024]{2,1,0:T(8,128)(2,1)} %param.12), kind=kOutput, calls=%fused_computation.23 | convolution fusion | flops 13428326400 | bytes 23855104 | tf_op jit(solution)/shard_map/transpose(jvp())/dot_general | solution.py:10
  218.3 25.8 %all-gather.23.cloned.1.call-done = bf16[1,1024,3200]{2,1,0:T(8,128)(2,1)} async-done(((bf16[1,128,3200]{2,1,0:T(8,128)(2,1)}), bf16[1,1024,3200]{2,1,0:T(8,128)(2,1)}) %all-gather.23.cloned.1.call-update) | async-done | bytes 6553616 | tf_op jit(solution)/shard_map/all_gather | solution.py:35
  244.1 22.8 %fusion.28 = f32[2048,3200]{1,0:T(8,128)} fusion(bf16[1,1024,3200]{2,1,0:T(8,128)(2,1)} %all-gather.23.cloned.1.call-done, bf16[2048,1024]{0,1:T(8,128)(2,1)} %get-tuple-element.33, f32[2048]{0:T(1024)S(1)} %fusion.74), kind=kOutput, calls=%fused_computation.46 | convolution fusion | flops 13428064256 | bytes 36970496 | tf_op jit(solution)/shard_map/jvp()/dot_general | solution.py:22
  266.9 24.0 %all-gather.19.cloned.1.call-done = bf16[1,1024,3200]{2,1,0:T(8,128)(2,1)} async-done(((bf16[1,128,3200]{2,1,0:T(8,128)(2,1)}), bf16[1,1024,3200]{2,1,0:T(8,128)(2,1)}) %all-gather.19.cloned.1.call-update) | async-done | bytes 6553616 | tf_op jit(solution)/shard_map/all_gather | solution.py:35
  290.8 38.8 %fusion.2 = (bf16[2048,3200]{1,0:T(8,128)(2,1)}, f32[2048,3200]{1,0:T(8,128)}) fusion(f32[2048,3200]{1,0:T(8,128)} %fusion.28, bf16[2048,3200]{1,0:T(8,128)(2,1)} %convolution_convert_fusion.1, bf16[1,1024,3200]{2,1,0:T(8,128)(2,1)} %all-gather.19.cloned.1.call-done, bf16[2048,1024]{0,1:T(8,128)(2,1)} %get-tuple-element.33, f32[2048]{0:T(1024)S(1)} %fusion.74), kind=kOutput, calls=%fused_computation.8 | convolution fusion | flops 13506707456 | bytes 89399296 | tf_op jit(solution)/shard_map/jvp()/dot_general | solution.py:21
  329.7 22.6 %fusion.12 = bf16[2048,1024]{0,1:T(8,128)(2,1)} fusion(bf16[2048,3200]{1,0:T(8,128)(2,1)} %convolution_convert_fusion.1, bf16[1,1024,3200]{2,1,0:T(8,128)(2,1)} %all-gather.23.cloned.1.call-done, f32[2048,3200]{1,0:T(8,128)} %get-tuple-element.35), kind=kOutput, calls=%fused_computation.21 | convolution fusion | flops 13461094400 | bytes 50069504 | tf_op jit(solution)/shard_map/transpose(jvp())/dot_general | solution.py:22
  352.2 21.8 %fusion.21 = (f32[2048]{0:T(1024)S(1)}, bf16[2048,1024]{0,1:T(8,128)(2,1)}) fusion(bf16[2048,1024]{0,1:T(8,128)(2,1)S(1)} %copy-done.6, bf16[2048,1024]{0,1:T(8,128)(2,1)} %fusion.12, bf16[2048,3200]{1,0:T(8,128)(2,1)} %get-tuple-element.34, bf16[1,1024,3200]{2,1,0:T(8,128)(2,1)} %all-gather.19.cloned.1.call-done), kind=kOutput, calls=%fused_computation.39 | convolution fusion | flops 13432256512 | bytes 32251904 | tf_op jit(solution)/shard_map/transpose(jvp())/dot_general | solution.py:21
  374.1 4.9 fusion.44
  379.0 2.1 copy-done.7
  381.0 19.5 %convolution_convert_fusion.2 = bf16[3200,1024]{1,0:T(8,128)(2,1)} fusion(bf16[2048,3200]{1,0:T(8,128)(2,1)} %get-tuple-element.30, bf16[2048,1024]{0,1:T(8,128)(2,1)S(1)} %fusion.44), kind=kOutput, calls=%fused_computation.44 | convolution fusion | flops 13425049600 | bytes 23855104 | tf_op jit(solution)/shard_map/transpose(jvp())/dot_general | solution.py:10
  400.5 0.0 reduce-scatter.15.cloned.1.call-update
  400.6 0.0 reduce-scatter.17.cloned.1.call-start
  400.6 26.0 %fusion.25 = bf16[3200,1024]{1,0:T(8,128)(2,1)} fusion(f32[2048,3200]{1,0:T(8,128)} %fusion.28, bf16[1,2048,1024]{2,1,0:T(8,128)(2,1)} %param.12, f32[2048,3200]{1,0:T(8,128)} %get-tuple-element.35), kind=kOutput, calls=%fused_computation.41 | convolution fusion | flops 13464371200 | bytes 63176704 | tf_op jit(solution)/shard_map/transpose(jvp())/dot_general | solution.py:10
  426.7 0.0 reduce-scatter.11.cloned.1.call-start
  426.7 21.4 %convolution_convert_fusion = bf16[2048,3200]{1,0:T(8,128)(2,1)} fusion(bf16[2048,1024]{0,1:T(8,128)(2,1)} %copy-done.7, bf16[1,3200,1024]{2,1,0:T(8,128)(2,1)} %all-gather.17.cloned.1.call-done), kind=kOutput, calls=%fused_computation.22 | convolution fusion | flops 13428326400 | bytes 23855104 | tf_op jit(solution)/shard_map/transpose(jvp())/dot_general | solution.py:10
  448.2 24.3 %fusion.27 = bf16[1024,3200]{1,0:T(8,128)(2,1)} fusion(bf16[2048,3200]{1,0:T(8,128)(2,1)} %convolution_convert_fusion, f32[2048,3200]{1,0:T(8,128)} %fusion.41, bf16[1,2048,1024]{1,2,0:T(8,128)(2,1)S(1)} %copy-done.1, f32[2048]{0:T(1024)S(1)} %copy-done.19), kind=kOutput, calls=%fused_computation.43 | convolution fusion | flops 13470662656 | bytes 50077696 | tf_op jit(solution)/shard_map/transpose(jvp())/dot_general | solution.py:22
  472.5 0.0 reduce-scatter.13.cloned.1.call-start
  472.6 0.6 copy-done.15
  473.2 25.4 %fusion.26 = bf16[1024,3200]{1,0:T(8,128)(2,1)} fusion(bf16[2048,3200]{1,0:T(8,128)(2,1)} %convolution_convert_fusion.1, bf16[2048,1024]{0,1:T(8,128)(2,1)} %get-tuple-element.33, f32[2048]{0:T(1024)S(1)} %copy-done.15, f32[2048,3200]{1,0:T(8,128)} %get-tuple-element.35), kind=kOutput, calls=%fused_computation.42 | convolution fusion | flops 13470662656 | bytes 50077696 | tf_op jit(solution)/shard_map/transpose(jvp())/dot_general | solution.py:22
  498.6 0.0 reduce-scatter.7.cloned.1.call-start
  498.6 32.6 %fusion.22 = bf16[1024,3200]{1,0:T(8,128)(2,1)} fusion(f32[2048,3200]{1,0:T(8,128)} %fusion.41, f32[2048,3200]{1,0:T(8,128)} %get-tuple-element.31, bf16[2048,3200]{1,0:T(8,128)(2,1)} %convolution_convert_fusion, bf16[1,2048,1024]{1,2,0:T(8,128)(2,1)} %copy.20, f32[2048]{0:T(1024)S(1)} %copy-done.19), kind=kOutput, calls=%fused_computation.40 | convolution fusion | flops 13503430656 | bytes 76292096 | tf_op jit(solution)/shard_map/transpose(jvp())/dot_general | solution.py:21
  531.2 0.0 reduce-scatter.9.cloned.1.call-start
  531.3 21.0 %convolution_convert_fusion.3 = bf16[1024,3200]{1,0:T(8,128)(2,1)} fusion(bf16[2048,3200]{1,0:T(8,128)(2,1)} %get-tuple-element.34, bf16[2048,1024]{0,1:T(8,128)(2,1)} %get-tuple-element.33, f32[2048]{0:T(1024)S(1)} %copy-done.15), kind=kOutput, calls=%fused_computation.45 | convolution fusion | flops 13428064256 | bytes 23863296 | tf_op jit(solution)/shard_map/transpose(jvp())/dot_general | solution.py:21
  552.3 0.0 all-reduce.3.cloned.1.call-start
  552.4 0.0 reduce-scatter.15.cloned.1.call-done
  552.4 0.0 reduce-scatter.17.cloned.1.call-done
  552.4 0.0 reduce-scatter.11.cloned.1.call-done
  552.5 39.2 %reduce-scatter.13.cloned.1.call-done = bf16[128,3200]{1,0:T(8,128)(2,1)} async-done(((bf16[1024,3200]{1,0:T(8,128)(2,1)}), bf16[128,3200]{1,0:T(8,128)(2,1)}) %reduce-scatter.13.cloned.1.call-update) | async-done | bytes 819216 | tf_op jit(solution)/shard_map/reduce_scatter | solution.py:38
  591.6 48.6 %reduce-scatter.7.cloned.1.call-done = bf16[128,3200]{1,0:T(8,128)(2,1)} async-done(((bf16[1024,3200]{1,0:T(8,128)(2,1)}), bf16[128,3200]{1,0:T(8,128)(2,1)}) %reduce-scatter.7.cloned.1.call-update) | async-done | bytes 819216 | tf_op jit(solution)/shard_map/reduce_scatter | solution.py:38
  640.3 48.5 %reduce-scatter.9.cloned.1.call-done = bf16[128,3200]{1,0:T(8,128)(2,1)} async-done(((bf16[1024,3200]{1,0:T(8,128)(2,1)}), bf16[128,3200]{1,0:T(8,128)(2,1)}) %reduce-scatter.9.cloned.1.call-update) | async-done | bytes 819216 | tf_op jit(solution)/shard_map/reduce_scatter | solution.py:38
  688.8 175.6 %all-reduce.3.cloned.1.call-done = (bf16[1,128,3200]{2,1,0:T(8,128)(2,1)}, bf16[1,128,3200]{2,1,0:T(8,128)(2,1)}, bf16[1,128,3200]{2,1,0:T(8,128)(2,1)}, bf16[1,...) async-done(((bf16[1,128,3200]{2,1,0:T(8,128)(2,1)}, bf16[1,128,3200]{2,1,0:T(8,128)(2,1)}, bf16[1,128,3200]{2,1,0:T(8,128)(2,1)}, ...) | async-done | bytes 4915216 | tf_op jit(solution)/shard_map/psum | solution.py:38
  864.4 7.4 fusion.61
  871.8 0.3 copy-done.8
  872.1 1.4 copy-done.9
  873.5 0.9 copy-done.10
  874.4 0.9 copy-done.11
  875.4 0.1 copy-done.12
  875.5 0.2 copy-done.13
  875.7 8.7 fusion.53
  (42 shorter events, 0.2 us)
Async XLA Ops:
  7.2 5.7 copy-start.2
  7.2 49.6 %all-gather.13.cloned.1.call-start = ((), (), s32[]{:S(2)}) async-start(), calls=%async_computation.12 | async-start | bytes 7372800 | tf_op jit(solution)/shard_map/all_gather | solution.py:35
  10.0 93.7 %all-gather.15.cloned.1.call-start = ((), (), s32[]{:S(2)}) async-start(), calls=%async_computation.13 | async-start | bytes 7372800 | tf_op jit(solution)/shard_map/all_gather | solution.py:35
  12.8 137.8 %all-gather.17.cloned.1.call-start = ((), (), s32[]{:S(2)}) async-start(), calls=%async_computation.14 | async-start | bytes 7372800 | tf_op jit(solution)/shard_map/all_gather | solution.py:35
  14.2 183.2 %all-gather.21.cloned.1.call-start = ((), (), s32[]{:S(2)}) async-start(), calls=%async_computation.16 | async-start | bytes 7372800 | tf_op jit(solution)/shard_map/all_gather | solution.py:35
  14.7 229.4 %all-gather.23.cloned.1.call-start = ((), (), s32[]{:S(2)}) async-start(), calls=%async_computation.17 | async-start | bytes 7372800 | tf_op jit(solution)/shard_map/all_gather | solution.py:35
  15.3 275.5 %all-gather.19.cloned.1.call-start = ((), (), s32[]{:S(2)}) async-start(), calls=%async_computation.15 | async-start | bytes 7372800 | tf_op jit(solution)/shard_map/all_gather | solution.py:35
  15.9 536.5 %reduce-scatter.15.cloned.1.call-start = ((), (), s32[]{:S(2)}) async-start(), calls=%async_computation.10 | async-start | bytes 7372800 | tf_op jit(solution)/shard_map/reduce_scatter | solution.py:38
  25.6 78.2 %copy-start.18 = (f32[2048]{0:T(1024)}, f32[2048]{0:T(1024)S(1)}, u32[]{:S(2)}) copy-start(f32[2048]{0:T(1024)S(1)} %add_rsqrt_fusion) | copy-start | bytes 24580
  172.5 45.8 %copy-start.16 = (f32[2048]{0:T(1024)}, f32[2048]{0:T(1024)S(1)}, u32[]{:S(2)}) copy-start(f32[2048]{0:T(1024)S(1)} %get-tuple-element.32) | copy-start | bytes 24580
  172.5 201.5 %copy-start.14 = (f32[2048]{0:T(1024)}, f32[2048]{0:T(1024)S(1)}, u32[]{:S(2)}) copy-start(f32[2048]{0:T(1024)S(1)} %fusion.74) | copy-start | bytes 24580
  329.7 22.6 %copy-start.6 = (bf16[2048,1024]{0,1:T(8,128)(2,1)S(1)}, bf16[2048,1024]{0,1:T(8,128)(2,1)}, u32[]{:S(2)}) copy-start(bf16[2048,1024]{0,1:T(8,128)(2,1)} %get-tuple-element.33) | copy-start | bytes 12582916
  352.2 21.8 %copy-start.17 = (f32[2048]{0:T(1024)S(1)}, f32[2048]{0:T(1024)}, u32[]{:S(2)}) copy-start(f32[2048]{0:T(1024)} %copy-done.16) | copy-start | bytes 24580
  352.2 21.8 %copy-start = (bf16[1,2048,1024]{1,2,0:T(8,128)(2,1)S(1)}, bf16[1,2048,1024]{1,2,0:T(8,128)(2,1)}, u32[]{:S(2)}) copy-start(bf16[1,2048,1024]{1,2,0:T(8,128)(2,1)} %copy.21) | copy-start | bytes 12582916
  379.0 2.1 copy-start.7
  400.6 151.9 %reduce-scatter.17.cloned.1.call-start = ((), (), s32[]{:S(2)}) async-start(), calls=%async_computation.11 | async-start | bytes 7372800 | tf_op jit(solution)/shard_map/reduce_scatter | solution.py:38
  426.6 21.5 %copy-start.19 = (f32[2048]{0:T(1024)S(1)}, f32[2048]{0:T(1024)}, u32[]{:S(2)}) copy-start(f32[2048]{0:T(1024)} %copy-done.18) | copy-start | bytes 24580
  426.7 125.8 %reduce-scatter.11.cloned.1.call-start = ((), (), s32[]{:S(2)}) async-start(), calls=%async_computation.8 | async-start | bytes 7372800 | tf_op jit(solution)/shard_map/reduce_scatter | solution.py:38
  426.7 21.5 %copy-start.1 = (bf16[1,2048,1024]{1,2,0:T(8,128)(2,1)S(1)}, bf16[1,2048,1024]{1,2,0:T(8,128)(2,1)}, u32[]{:S(2)}) copy-start(bf16[1,2048,1024]{1,2,0:T(8,128)(2,1)} %copy.20) | copy-start | bytes 12582916
  472.5 0.7 copy-start.15
  472.5 119.1 %reduce-scatter.13.cloned.1.call-start = ((), (), s32[]{:S(2)}) async-start(), calls=%async_computation.9 | async-start | bytes 7372800 | tf_op jit(solution)/shard_map/reduce_scatter | solution.py:38
  498.6 141.7 %reduce-scatter.7.cloned.1.call-start = ((), (), s32[]{:S(2)}) async-start(), calls=%async_computation.6 | async-start | bytes 7372800 | tf_op jit(solution)/shard_map/reduce_scatter | solution.py:38
  531.2 157.5 %reduce-scatter.9.cloned.1.call-start = ((), (), s32[]{:S(2)}) async-start(), calls=%async_computation.7 | async-start | bytes 7372800 | tf_op jit(solution)/shard_map/reduce_scatter | solution.py:38
  552.3 312.0 %copy-start.3 = (bf16[2,400,1024]{2,1,0:T(8,128)(2,1)S(1)}, bf16[2,400,1024]{2,1,0:T(8,128)(2,1)}, u32[]{:S(2)}) copy-start(bf16[2,400,1024]{2,1,0:T(8,128)(2,1)} %param.15) | copy-start | bytes 4915204
  552.3 312.0 %all-reduce.3.cloned.1.call-start = ((), (), s32[]{:S(2)}) async-start(), calls=%async_computation.18 | async-start | bytes 9830400 | tf_op jit(solution)/shard_map/psum | solution.py:38
  864.3 7.4 copy-start.4
  864.3 7.4 copy-start.5
  864.3 7.7 copy-start.8
  864.3 9.2 %copy-start.9 = (f32[2,128,3200]{2,1,0:T(8,128)S(1)}, f32[2,128,3200]{2,1,0:T(8,128)}, u32[]{:S(2)}) copy-start(f32[2,128,3200]{2,1,0:T(8,128)} %param.16) | copy-start | bytes 9830404
  864.3 10.1 %copy-start.10 = (f32[2,128,3200]{2,1,0:T(8,128)S(1)}, f32[2,128,3200]{2,1,0:T(8,128)}, u32[]{:S(2)}) copy-start(f32[2,128,3200]{2,1,0:T(8,128)} %param.20) | copy-start | bytes 9830404
  864.4 11.0 %copy-start.11 = (f32[2,128,3200]{2,1,0:T(8,128)S(1)}, f32[2,128,3200]{2,1,0:T(8,128)}, u32[]{:S(2)}) copy-start(f32[2,128,3200]{2,1,0:T(8,128)} %param.17) | copy-start | bytes 9830404
  864.4 11.1 %copy-start.12 = (bf16[1,128,3200]{2,1,0:T(8,128)(2,1)S(1)}, bf16[1,128,3200]{2,1,0:T(8,128)(2,1)}, u32[]{:S(2)}) copy-start(bf16[1,128,3200]{2,1,0:T(8,128)(2,1)} %get-tuple-element.9) | copy-start | bytes 2457604
  864.4 11.4 %copy-start.13 = (bf16[1,128,3200]{2,1,0:T(8,128)(2,1)S(1)}, bf16[1,128,3200]{2,1,0:T(8,128)(2,1)}, u32[]{:S(2)}) copy-start(bf16[1,128,3200]{2,1,0:T(8,128)(2,1)} %get-tuple-element.10) | copy-start | bytes 2457604
Sparse Core Ops, SparseCore 0:
  10.4 46.3 all-gather.12
  59.2 44.4 all-gather.14
  106.1 44.4 all-gather.16
  152.9 44.4 all-gather.20
  199.6 44.4 all-gather.22
  246.3 44.4 all-gather.18
  400.7 45.1 reduce-scatter.14
  448.5 46.0 reduce-scatter.16
  497.1 46.0 reduce-scatter.10
  545.6 46.0 reduce-scatter.12
  594.2 46.0 reduce-scatter.6
  642.7 46.0 reduce-scatter.8
  693.0 171.3 all-reduce.2
where the time goes:
time: 899 us; the launch traced here: 891 us
  waiting for transfers between devices  452 us (50%)
  matrix products  373 us (41%)
  local copies, waits for them, and re-layouts  26.5 us (3%)
  other arithmetic  24 us (3%)
  between operations  14.3 us (2%)
    psum x1, waiting for transfers between devices, summed(): lax.psum(lax.psum_scatter(term, 's', scatter_dimension=0, tiled=True), 'r')  176 us
    all_gather x6, waiting for transfers between devices, fetched(): lax.all_gather(w[number], 's', axis=0, tiled=True)  139 us
    dot_general x5, matrix products, layer(): gate = jnp.dot(a, w['w_gate'], preferred_element_type=jnp.float32)  137 us
    reduce_scatter x6, waiting for transfers between devices, summed(): lax.psum_scatter(term, 's', scatter_dimension=0, tiled=True)  136 us
    dot_general x5, matrix products, layer(): up = jnp.dot(a, w['w_up'], preferred_element_type=jnp.float32)  126 us
    dot_general x5, matrix products, matmul(): jnp.dot(a, w, preferred_element_type=jnp.float32).astype(jnp.bfloat16)  110 us
    unnamed x42, local copies, waits for them, and re-layouts  19.8 us
  transfers between devices with their start and end apart: 13, of which 10 were waited for; matrix products, arithmetic and copies ran while one was open for 33% of the time, Pallas kernels for 0%

commit v1 on v0

v1 whole, which is shorter than its diff:
```python
import jax
import jax.numpy as jnp
from jax import lax
from jax.experimental import pallas as pl
from jax.experimental.pallas import tpu as pltpu
from jax.sharding import PartitionSpec as P

BF, F32 = jnp.bfloat16, jnp.float32
NN, NT = (((1,), (0,)), ((), ())), (((1,), (1,)), ((), ()))
DMA, V, S = pltpu.SemaphoreType.DMA, pltpu.VMEM, jax.ShapeDtypeStruct
ANY = pl.BlockSpec(memory_space=pl.ANY)
LIMIT = 67_043_328
LAYERS, CORES, NX, NY, NZ = 2, 2, 4, 4, 8
SHARDS = NX * CORES
T, D, F = 2048, 1024, 3200
LANES, W, HALF, GROUP = 128, 256, 1024, 512
TILES = -(-F // W)
LAST = TILES - 1
GR, DR = D // SHARDS, F // SHARDS
PAIR = 2
ROWS = 256


def par(i):
    return lax.rem(i, PAIR)


def seg(i, n, step=None):
    return pl.ds(pl.multiple_of(i * (n if step is None else step), n), n)


def off(j):
    return pl.multiple_of(W * j - (TILES * W - F) * (j // LAST), LANES)


def tile_cols(j):
    return pl.ds(off(j), W)


def dot(a, b, dn=NN):
    return lax.dot_general(a, b, dn, preferred_element_type=F32)


def fetch(src, dst, sem):
    return pltpu.make_async_copy(src, dst, sem)


def start(copies):
    for c in copies:
        c.start()


def done(copies):
    for c in copies:
        c.wait()


def got(copies):
    for c in copies:
        c.wait_recv()


def sent(copies):
    for c in copies:
        c.wait_send()


def norm_of(h):
    wide = h.astype(F32)
    return wide, lax.rsqrt(jnp.mean(wide * wide, -1, keepdims=True) + 1e-6)


class Place:
    def __init__(self):
        r, s = lax.axis_index("r"), lax.axis_index("s")
        self.x, self.c, self.y, self.z = s // CORES, lax.rem(s, CORES), r // NZ, lax.rem(r, NZ)
        self.me = s

    def at(self, x, y, z, c):
        return {"r": y * NZ + z, "s": x * CORES + c}

    def along(self, axis, d):
        if axis == "x":
            return self.at(lax.rem(self.x + d, NX), self.y, self.z, self.c)
        if axis == "y":
            return self.at(self.x, lax.rem(self.y + d, NY), self.z, self.c)
        return self.at(self.x, self.y, lax.rem(self.z + d, NZ), self.c)

    def sib(self):
        return self.at(self.x, self.y, self.z, 1 - self.c)

    def greet(self):
        bar = pltpu.get_barrier_semaphore()
        peers = [self.sib()] + [self.along(a, d) for a, n in SIZES.items() for d in range(1, n)]
        for q in peers:
            pl.semaphore_signal(bar, inc=1, device_id=q, device_id_type=pl.DeviceIdType.MESH)
        pl.semaphore_wait(bar, len(peers))


SIZES = {"x": NX, "y": NY, "z": NZ}


def rcopy(src, dst, ss, rs, to):
    return pltpu.make_async_remote_copy(src, dst, ss, rs, device_id=to, device_id_type=pl.DeviceIdType.MESH)


class Gather:
    def __init__(self, route, first, width, gu):
        self.route, self.first, self.width, self.gu = route, first, width, gu

    def scratch(self):
        n = SIZES[self.route] if self.route != "x" else CORES
        return [DMA((PAIR, NX)), DMA((PAIR, n, NX)), DMA((PAIR, NX)), DMA((1,))]

    def bind(self, p, refs, own, full):
        self.p, self.own, self.full = p, own, full
        self.a, self.b, self.c, self.l = refs
        return self

    def whole(self):
        return (slice(None), pl.ds(self.first, self.width))

    def piece(self):
        q, n = (self.p.y, NY) if self.route == "y" else (self.p.z, NZ)
        if self.gu:
            return (seg(q, GR // n), pl.ds(self.first, self.width))
        n = self.width // n
        return (slice(None), pl.ds(pl.multiple_of(self.first + q * n, n), n))

    def mine(self, where):
        return self.own.at[(slice(None),) + where] if self.gu else self.own.at[where]

    def block(self, s, where):
        return self.full.at[(slice(None), s) + where] if self.gu else self.full.at[(s,) + where]

    def shard(self, k):
        return CORES * lax.rem(self.p.x + k, NX) + self.p.c

    def A(self):
        where = self.whole() if self.route == "x" else self.piece()
        return [rcopy(self.mine(where), self.block(self.p.me, where), self.a.at[0, d], self.a.at[1, d], self.p.along("x", d)) for d in range(1, NX)]

    def B(self):
        out, where = [], self.piece()
        for k in range(1, NX):
            b = self.block(self.shard(k), where)
            out += [rcopy(b, b, self.b.at[0, d, k], self.b.at[1, d, k], self.p.along(self.route, d)) for d in range(1, SIZES[self.route])]
        return out

    def O(self):
        w = self.whole()
        return [rcopy(self.mine(w), self.block(self.p.me, w), self.c.at[0, 0], self.c.at[1, 0], self.p.sib())]

    def C(self):
        out = []
        for k in range(1, NX):
            b = self.block(self.shard(k), self.whole())
            out.append(rcopy(b, b, self.c.at[0, k], self.c.at[1, k], self.p.sib()))
        return out

    def local(self):
        w = self.whole()
        return [fetch(self.mine(w), self.block(self.p.me, w), self.l.at[0])]

    def go(self):
        start(self.A() + self.O() + self.local())

    def pass_on(self):
        got(self.A())
        start(self.B())

    def share(self):
        got(self.A() if self.route == "x" else self.B())
        start(self.C())

    def ready(self):
        got(self.C() + self.O())
        done(self.local())

    def finish(self):
        sent(self.A() + self.O() + self.C() + (self.B() if self.route != "x" else []))


def gu_parts():
    return [Gather(r, f, w, True) for r, f, w in (("x", 0, W), ("x", W, W), ("y", 512, 512), ("y", 1024, 512), ("y", 1536, 768), ("z", 2304, 896))]


def down_parts(first):
    return [Gather(r, f, GROUP, False) for r, f in ((first, 0), ("y", GROUP))]


def refs_of(parts, refs):
    n = len(parts[0].scratch())
    return [refs[n * i:n * i + n] for i in range(len(parts))]


class Engine:
    def __init__(self, gu, ring):
        self.gu, self.ring, self.routes = gu, ring, ("x", "y") if gu else ("x", "x")
        self.R, self.C = (GR, W) if gu else (DR, LANES)
        self.P = 32 if gu else LANES
        self.zr = self.P // (PAIR if gu else NX)

    def scratch(self):
        R, C, Q, n = self.R, self.C, self.P, self.ring
        half = (PAIR, NX, R, C) if self.gu else (NX, R, PAIR * C)
        first = [V((n, NX - 1, R, C) if r == "x" else (n, NY - 1, NX, Q, C), BF) for r in self.routes]
        then = [V((PAIR, NY * Q, C) if r == "x" else (PAIR, NX, Q, C), BF) for r in self.routes]
        part = (NZ, self.zr, LANES)
        nd = 1 if self.gu else NX
        sems = [(PAIR, nd), (PAIR, nd)]
        for k in ((PAIR, NX), (PAIR, NX), (NZ,), (NZ,), (NY,)):
            sems += [(PAIR,) + k, (n,) + k]
        return ([V((PAIR,) + half, BF), V((PAIR, PAIR, NX, R, C), BF)] + first + then
                + [V((n, PAIR, NX - 1, Q, C), BF), V((PAIR,) + part, BF), V((n,) + part, BF), V((n,) + part, BF)]
                + [V((PAIR, PAIR, Q, C) if self.gu else (PAIR, Q, PAIR * C), BF)]
                + [DMA(s) for s in sems + [(PAIR,)]])

    REFS = 24

    def bind(self, p, refs, own, src, out_at):
        self.p, self.own, self.src, self.out_at = p, own, src, out_at
        (self.rS, self.XS, a, b, ya, yb, self.R2, self.Zp, self.R3, self.ZG, self.YS,
         self.s0, self.r0, self.s1, self.r1, self.s2, self.r2, self.s3, self.r3, self.s4, self.r4, self.s5, self.r5, self.so) = refs
        self.R1, self.Y = (a, b), (ya, yb)
        if not self.gu:
            for y in self.Y:
                for k in range(PAIR):
                    y[k, DR:] = jnp.zeros((NY * self.P - DR, self.C), BF)

    def slot(self, it):
        return lax.rem(it, self.ring)

    def c0(self, it):
        k, n = par(it), (1 if self.gu else NX)
        return [rcopy(self.src(it, i), self.rS.at[k] if self.gu else self.rS.at[k, i], self.s0.at[k, i], self.r0.at[k, i], self.p.sib()) for i in range(n)]

    def ypart(self, y):
        return seg(y, self.P)

    def c1(self, it):
        k, n, p, out = par(it), self.slot(it), self.p, []
        for d in range(1, NX):
            for m, route in enumerate(self.routes):
                src = self.XS.at[k, m, lax.rem(p.x + d, NX)] if route == "x" else self.XS.at[k, m, :, self.ypart(lax.rem(p.y + d, NY))]
                out.append(rcopy(src, self.R1[m].at[n, d - 1], self.s1.at[k, m, d], self.r1.at[n, m, d], p.along(route, d)))
        return out

    def c2(self, it):
        k, n, p, out = par(it), self.slot(it), self.p, []
        for d in range(1, NX):
            for m, route in enumerate(self.routes):
                src = self.Y[m].at[k, self.ypart(lax.rem(p.y + d, NY))] if route == "x" else self.Y[m].at[k, lax.rem(p.x + d, NX)]
                out.append(rcopy(src, self.R2.at[n, m, d - 1], self.s2.at[k, m, d], self.r2.at[n, m, d], p.along("y" if route == "x" else "x", d)))
        return out

    def c3(self, it):
        k, n, p = par(it), self.slot(it), self.p
        return [rcopy(self.Zp.at[k, lax.rem(p.z + d, NZ)], self.R3.at[n, d], self.s3.at[k, d], self.r3.at[n, d], p.along("z", d)) for d in range(1, NZ)]

    def c4(self, it):
        k, n, p = par(it), self.slot(it), self.p
        b = self.ZG.at[n, p.z]
        return [rcopy(b, b, self.s4.at[k, d], self.r4.at[n, d], p.along("z", d)) for d in range(1, NZ)]

    def c5(self, it, src, dst):
        k, n = par(it), self.slot(it)
        return [rcopy(src, dst, self.s5.at[k, d], self.r5.at[n, d], self.p.along("y", d)) for d in range(1, NY)]

    def out(self, it, f):
        for cond, src, dst in self.out_at(it):
            @pl.when(cond)
            def _():
                f(src, dst)

    def left(self, it, k):
        if k < 5:
            return sent((self.c0, self.c1, self.c2, self.c3, self.c4)[k](it))

        def f(src, dst):
            sent(self.c5(it, src, dst))
            fetch(src, dst, self.so.at[par(it)]).wait()
        self.out(it, f)

    def free(self, it, k):
        @pl.when(it >= PAIR)
        def _():
            self.left(it - PAIR, k)

    def S0(self, it):
        start(self.c0(it))

    def S1(self, it):
        k, C = par(it), self.C
        got(self.c0(it))
        self.free(it, 1)

        def add(xx, _):
            for m in range(PAIR):
                other = self.rS[k, m, xx] if self.gu else self.rS[k, xx, :, m * C:m * C + C]
                self.XS[k, m, xx] = (self.own(it, m, xx).astype(F32) + other.astype(F32)).astype(BF)
            return 0
        lax.fori_loop(0, NX, add, 0)
        start(self.c1(it))

    def S2(self, it):
        k, n, p = par(it), self.slot(it), self.p
        got(self.c1(it))
        self.free(it, 2)
        for m, route in enumerate(self.routes):
            t = (self.XS[k, m, p.x] if route == "x" else self.XS[k, m, :, self.ypart(p.y)]).astype(F32)
            for d in range(NX - 1):
                t = t + self.R1[m][n, d].astype(F32)
            if route == "x":
                self.Y[m][k, :self.R] = t.astype(BF)
            else:
                self.Y[m][k] = t.astype(BF)
        start(self.c2(it))

    def S3(self, it):
        k, n, p = par(it), self.slot(it), self.p
        got(self.c2(it))
        self.free(it, 3)
        for m, route in enumerate(self.routes):
            t = (self.Y[m][k, self.ypart(p.y)] if route == "x" else self.Y[m][k, p.x]).astype(F32)
            for d in range(NY - 1):
                t = t + self.R2[n, m, d].astype(F32)
            t = t.astype(BF)
            for q in range(NX):
                self.Zp[k, m * NX + q] = t[self.quarter(q)]
        start(self.c3(it))

    def quarter(self, q):
        z = self.zr
        if not self.gu:
            return (slice(z * q, z * q + z), slice(None))
        a, b = z * (q // PAIR), LANES * (q % PAIR)
        return (slice(a, a + z), slice(b, b + LANES))

    def S4(self, it):
        k, n, p = par(it), self.slot(it), self.p
        got(self.c3(it))
        self.free(it, 4)
        t = self.Zp[k, p.z].astype(F32)
        for d in range(1, NZ):
            t = t + self.R3[n, d].astype(F32)
        self.ZG[n, p.z] = t.astype(BF)
        start(self.c4(it))

    def S5(self, it):
        k, n = par(it), self.slot(it)
        got(self.c4(it))
        self.free(it, 5)
        for q in range(NZ):
            m, (a, b) = q // NX, self.quarter(q % NX)
            if self.gu:
                self.YS[k, m, a, b] = self.ZG[n, q]
            else:
                self.YS[k, a, m * LANES:m * LANES + LANES] = self.ZG[n, q]

        def f(src, dst):
            start(self.c5(it, src, dst) + [fetch(src, dst, self.so.at[k])])
        self.out(it, f)

    def S6(self, it):
        self.out(it, lambda src, dst: got(self.c5(it, src, dst)))

    def stage(self, k, there, it):
        @pl.when(there)
        def _():
            (self.S0, self.S1, self.S2, self.S3, self.S4, self.S5, self.S6)[k](it)

    def finish(self, items):
        for it in range(items - PAIR, items):
            for k in range(6):
                self.left(jnp.int32(it), k)


OFFS = (0, 1, 3, 5, 7, 9, 11)
LATER = (6, 5, 4, 3, 2)
WIDE_STEPS = NORM_STEPS = 4
AT_DOWN1 = TILES
AT_NORM = AT_DOWN1 + WIDE_STEPS
AT_DOWN0 = AT_NORM + NORM_STEPS
AT_TILES0 = AT_DOWN0 + WIDE_STEPS
STEPS = AT_TILES0 + TILES + OFFS[-1]
DN_STRIDE, DN_EACH = 2, D // W
DN_ITEMS = LAYERS * DN_EACH


def gu_item(u):
    v = lax.max(u, 0)
    return ((u >= 0) & (v < TILES)) | ((v >= AT_TILES0) & (v < AT_TILES0 + TILES)), v - (AT_TILES0 - TILES) * (v // AT_TILES0)


def dn_item(u):
    v = lax.max(u - AT_NORM, 0)
    return (u >= AT_NORM) & (lax.rem(v, DN_STRIDE) == 0) & (v < DN_STRIDE * DN_ITEMS), v // DN_STRIDE


class Down:
    def __init__(self, p, act_hs, dhT, h, ab, buf, town, s_a, s_o, s_t):
        self.p, self.act_hs, self.dhT, self.h, self.ab, self.buf, self.town = p, act_hs, dhT, h, ab, buf, town
        self.s_a, self.s_o, self.s_t = s_a, s_o, s_t

    def run(self, n, i):
        def load(q):
            return fetch(self.act_hs[n].at[q], self.ab.at[par(q)], self.s_a.at[par(q)])

        def store(q):
            return fetch(self.buf, self.h.at[n, tile_cols(q)], self.s_o.at[0])
        lo, each = 3 * i + lax.min(i, 1), 3 + (i == 0).astype(jnp.int32)

        def step(q, _):
            @pl.when(q == 0)
            def _():
                load(q).start()

            @pl.when(q + 1 < TILES)
            def _():
                load(q + 1).start()
            load(q).wait()
            t = dot(self.dhT[...], self.ab[par(q)]).astype(BF).T

            @pl.when(q > lo)
            def _():
                store(q - 1).wait()
            self.buf[...] = t
            store(q).start()
            return 0
        lax.fori_loop(lo, lo + each, step, 0)
        store(lo + each - 1).wait()

    def block(self, it, k, c):
        return self.h.at[it // DN_EACH, pl.ds(pl.multiple_of(DR * (CORES * k + c), 16), DR), seg(lax.rem(it, DN_EACH), W)]

    def src(self, it, k):
        return self.block(it, k, 1 - self.p.c)

    def mine(self, it):
        return [fetch(self.block(it, k, self.p.c), self.town.at[k], self.s_t.at[k]) for k in range(NX)]

    def own(self, it, m, xx):
        return self.town[xx, :, m * LANES:m * LANES + LANES]

    def hook(self, eng, i):
        for k in LATER:
            eng.stage(k, *dn_item(i - OFFS[k]))
        there, it = dn_item(i - OFFS[1])

        @pl.when(there)
        def _():
            done(self.mine(it))
            eng.S1(it)
        there0, it0 = dn_item(i)

        @pl.when(there0)
        def _():
            eng.free(it0, 0)
            start(self.mine(it0))
            eng.S0(it0)


class Sums:
    def __init__(self):
        self.gu, self.dn = Engine(True, 4), Engine(False, 2)

    def scratch(self):
        return [V((PAIR, PAIR, NX, CORES, GR, W), BF)] + self.gu.scratch() + self.dn.scratch()

    def bind(self, p, refs, gu_h, dn_h, down):
        n = Engine.REFS
        self.t, self.down = refs[0], down

        def gu_out(it):
            l, j, r, e = 1 - it // TILES, lax.rem(it, TILES), seg(p.y, 32), self.gu.YS.at[par(it)]
            return [(j < LAST, e, gu_h.at[:, l, r, seg(j, W)]), (j == LAST, e.at[:, :, LANES:], gu_h.at[:, l, r, pl.ds(F - LANES, LANES)])]

        def dn_out(it):
            return [(it >= 0, self.dn.YS.at[par(it)], dn_h.at[1 - it // DN_EACH, seg(p.y, LANES), seg(lax.rem(it, DN_EACH), W)])]
        self.gu.bind(p, refs[1:1 + n], lambda it, m, xx: self.t[par(it), m, xx, p.c], lambda it, k: self.t.at[par(it), :, :, 1 - p.c], gu_out)
        self.dn.bind(p, refs[1 + n:], down.own, down.src, dn_out)

    def put(self, it, m, aT, t):
        self.t[par(it), m] = dot(aT, t).astype(BF).reshape(NX, CORES, GR, W)

    def loop(self, tile1, put1, norm, before0, tile0, put0):
        def when(i, first, n, f):
            @pl.when((i >= first) & (i < first + n))
            def _():
                f(i - first)

        def step(i, _):
            for k in LATER:
                self.gu.stage(k, *gu_item(i - OFFS[k]))
            self.down.hook(self.dn, i)
            when(i, AT_DOWN1, WIDE_STEPS, lambda j: self.down.run(0, j))
            when(i, AT_NORM, NORM_STEPS, norm)
            when(i, AT_DOWN0 - 1, 1, before0)
            when(i, AT_DOWN0, WIDE_STEPS, lambda j: self.down.run(1, j))
            when(i, 0, TILES, tile1)
            when(i, AT_TILES0, TILES, tile0)
            self.gu.stage(1, *gu_item(i - OFFS[1]))
            when(i, 0, TILES, put1)
            when(i, AT_TILES0, TILES, put0)
            self.gu.stage(0, *gu_item(i))
            return 0
        lax.fori_loop(0, STEPS, step, 0)
        self.gu.finish(LAYERS * TILES)
        self.dn.finish(DN_ITEMS)


def hidden(d, g, u):
    sg = jax.nn.sigmoid(g)
    si = g * sg
    return si * u, d * u * (sg + si * (1 - sg)), d * si


def halves(part):
    lax.fori_loop(0, T // HALF, lambda i, _: (part(seg(i, HALF)), 0)[1], 0, unroll=True)


def stream(n, load, store, work):
    start(load(0))

    def step(i, _):
        @pl.when(i + 1 < n)
        def _():
            start(load(i + 1))
        done(load(i))

        @pl.when(i >= PAIR)
        def _():
            done(store(i - PAIR))
        work(i)
        start(store(i))
        return 0
    lax.fori_loop(0, n, step, 0)
    for i in range(n - PAIR, n):
        done(store(i))


def fa_parts():
    return gu_parts(), down_parts("x"), down_parts("y"), [Gather("x", 0, GROUP, True)]


def fa_kernel(*refs):
    (x_h, dy_h, wg_h, wu_h, wd_h, gu0_h, d0_h, d1_h, head_h, g_h, u_h, act_h, h1_h, a1_h, a1T_h, a0T_h, dyT_h,
     own0, own1, ownd, a, wd, act, wg, wu, gb, ub, xb, hb, ab, atb, s_own, s_w, s_b, s_act, s_x, s_o, s_wd), rest = refs[:38], refs[38:]
    p = Place()
    groups = fa_parts()
    every = [part for g in groups for part in g]
    for part, r, (own, full) in zip(every, refs_of(every, rest), [(own0, gu0_h)] * 6 + [(ownd.at[0], d0_h)] * 2 + [(ownd.at[1], d1_h)] * 2 + [(own1, head_h)]):
        part.bind(p, r, own, full)
    (x0, x1, y0, y1, y2, z0), (d0x, d0y), (d1a, d1b), (head,) = groups
    owns = [fetch(w.at[0], own0.at[k], s_own.at[k, 0]) for k, w in enumerate((wg_h, wu_h))]
    owns += [fetch(w.at[1, :, pl.ds(0, GROUP)], own1.at[k], s_own.at[k, 1]) for k, w in enumerate((wg_h, wu_h))]
    owns += [fetch(wd_h.at[k], ownd.at[k], s_own.at[CORES, k]) for k in range(LAYERS)]
    start(owns)
    p.greet()
    done(owns)
    for part in (y0, z0, x0, y1, x1, y2, d0y, d1a, d1b, d0x, head):
        part.go()
    n = T // GROUP

    def cut(i):
        return seg(i, GROUP)

    def first(i):
        wide, scale = norm_of(xb[par(i)])
        t = (wide * scale).astype(BF)
        a[cut(i)] = t
        atb[par(i)] = t.T

    def turn(i):
        atb[par(i)] = xb[par(i)].T

    def load(h):
        return lambda i: [fetch(h.at[cut(i)], xb.at[par(i)], s_x.at[par(i)])]

    def turned(h):
        return lambda i: [fetch(atb.at[par(i)], h.at[:, cut(i)], s_o.at[CORES, par(i)])]
    stream(n, load(x_h), turned(a0T_h), first)
    stream(n, load(dy_h), turned(dyT_h), turn)

    def wts(j):
        return [fetch(gu0_h.at[k, :, :, tile_cols(j)], w.at[par(j)], s_w.at[k, par(j)]) for k, w in enumerate((wg, wu))]

    def outs(j):
        return [fetch(b.at[par(j)], h.at[j], s_b.at[k, par(j)]) for k, (b, h) in enumerate(((gb, g_h), (ub, u_h)))]

    events = {
        0: [y0.pass_on, z0.pass_on, x0.share, x0.ready],
        1: [y1.pass_on, x1.share, x1.ready],
        2: [y2.pass_on, y0.share, y0.ready],
        4: [d0y.pass_on, y1.share, y1.ready],
        6: [d1a.pass_on, y2.share, y2.ready],
        9: [d1b.pass_on, z0.share, d0x.share, z0.ready],
    }

    def tile(j, _):
        k = par(j)
        for n_, todo in events.items():
            @pl.when(j == n_)
            def _():
                for f in todo:
                    f()
                start(wts(j))

        @pl.when(j + 1 < TILES)
        def _():
            ahead = j >= 0
            for n_ in events:
                ahead = ahead & (j + 1 != n_)

            @pl.when(ahead)
            def _():
                start(wts(j + 1))
        done(wts(j))

        @pl.when(j >= PAIR)
        def _():
            done(outs(j - PAIR))

        def part(r):
            g, u = dot(a[r], wg[k].reshape(D, W)), dot(a[r], wu[k].reshape(D, W))
            gb[k, r], ub[k, r] = g, u
            act[j, r] = (g * jax.nn.sigmoid(g) * u).astype(BF)
        halves(part)
        start(outs(j) + [fetch(act.at[j], act_h.at[j], s_act.at[j])])
        return 0
    lax.fori_loop(0, TILES, tile, 0)
    for j in range(TILES - PAIR, TILES):
        done(outs(j))
    d0y.share()
    head.share()
    d0x.ready()
    d0y.ready()
    wds = [fetch(d0_h.at[k], wd.at[pl.ds(DR * k, DR)], s_wd.at[k]) for k in range(SHARDS)]
    start(wds)
    d1a.share()
    d1b.share()
    done(wds)

    def down(i):
        k, r = par(i), cut(i)
        t = dot(act[LAST, r, LANES:], wd[F - LANES:])
        for j in range(LAST):
            t = t + dot(act[j, r], wd[W * j:W * j + W])
        h = xb[k] + t.astype(BF)
        wide, scale = norm_of(h)
        t = (wide * scale).astype(BF)
        hb[k], ab[k], atb[k] = h, t, t.T

    def finals(i):
        k, r = par(i), cut(i)
        return [fetch(hb.at[k], h1_h.at[r], s_o.at[0, k]), fetch(ab.at[k], a1_h.at[r], s_o.at[1, k]), fetch(atb.at[k], a1T_h.at[:, r], s_o.at[CORES, k])]
    stream(n, load(x_h), finals, down)
    done([fetch(act.at[j], act_h.at[j], s_act.at[j]) for j in range(TILES)])
    for part in (d1a, d1b, head):
        part.ready()
    for part in every:
        part.finish()


def params(number):
    return pltpu.CompilerParams(vmem_limit_bytes=LIMIT, collective_id=number, has_side_effects=True)


def cost(units):
    return pl.CostEstimate(flops=PAIR * units * T * D * F, bytes_accessed=LIMIT, transcendentals=T * F)


def slots(*shape, dtype=BF):
    return V((PAIR,) + shape, dtype)


def fa(x, dy, wg, wu, wd):
    tiles = lambda t: S((TILES, T, W), t)
    full = S((SHARDS, DR, D), BF)
    parts = [part for g in fa_parts() for part in g]
    return pl.pallas_call(
        fa_kernel, name="fa",
        out_shape=[S((PAIR, SHARDS, GR, F), BF), full, full, S((PAIR, SHARDS, GR, GROUP), BF), tiles(F32), tiles(F32), tiles(BF),
                   S((T, D), BF), S((T, D), BF), S((D, T), BF), S((D, T), BF), S((D, T), BF)],
        in_specs=[ANY] * 5, out_specs=[ANY] * 12,
        scratch_shapes=[slots(GR, F), slots(GR, GROUP), slots(DR, D), V((T, D), BF), V((F, D), BF), V((TILES, T, W), BF), slots(SHARDS, GR, W), slots(SHARDS, GR, W),
                        slots(T, W, dtype=F32), slots(T, W, dtype=F32), slots(GROUP, D), slots(GROUP, D), slots(GROUP, D), slots(D, GROUP),
                        DMA((3, 2)), DMA((2, 2)), DMA((2, 2)), DMA((TILES,)), DMA((2,)), DMA((3, 2)), DMA((SHARDS,))] + [s for part in parts for s in part.scratch()],
        compiler_params=params(1), cost_estimate=cost(3),
    )(x, dy, wg, wu, wd)


def bb_parts():
    return gu_parts()[2:]


def bb_kernel(*refs):
    (a_h, aT_h, dy_h, dyT_h, h_h, wg_h, wu_h, head_h, wd_h, a0T_h, act0_h, g_h, u_h, wd0_h, gu_h, dn_h, part_h, act_h, dg_h, du_h, w_h,
     a, aT, dy, dyT, da, own, wg, wu, wd, actb, dgb, dub, stage, town, hb, s_in, s_own, s_w, s_b, s_st, s_t, s_h), rest = refs[:43], refs[43:]
    p = Place()
    parts = bb_parts()
    n = sum(len(part.scratch()) for part in parts)
    for part, r in zip(parts, refs_of(parts, rest[:n])):
        part.bind(p, r, own, w_h)
    y0, y1, y2, z0 = parts
    down = Down(p, (act_h, act0_h), dyT, part_h, actb, stage, town, s_b.at[0], s_st, s_t)
    sums = Sums()
    sums.bind(p, rest[n:], gu_h, dn_h, down)
    owns = [fetch(w.at[1], own.at[k], s_own.at[k]) for k, w in enumerate((wg_h, wu_h))]
    ins = [fetch(h, v, s_in.at[k]) for k, (h, v) in enumerate(((a_h, a), (dy_h, dy), (aT_h, aT), (dyT_h, dyT)))]

    def wts(j, third):
        def of(w):
            return [fetch(w.at[k, :, :, tile_cols(j)], v.at[par(j)], s_w.at[k, par(j)]) for k, v in enumerate((wg, wu))]

        def both(f):
            @pl.when(j < PAIR)
            def _():
                f(of(head_h))

            @pl.when(j >= PAIR)
            def _():
                f(of(w_h))
            if third:
                f([fetch(wd_h.at[tile_cols(j)], wd.at[par(j)], s_w.at[CORES, par(j)])])
        return both
    bufs = ((actb, act_h), (dgb, dg_h), (dub, du_h))

    def outs(j):
        return [fetch(b.at[par(j)], h.at[j], s_b.at[k, par(j)]) for k, (b, h) in enumerate(bufs)]

    def back(j):
        return [fetch(h.at[j], b.at[par(j)], s_b.at[k, par(j)]) for k, (b, h) in enumerate(bufs) if k]
    start(owns + ins[:PAIR])
    p.greet()
    done(owns)
    for part in (y0, z0, y1, y2):
        part.go()
    start(ins[PAIR:])
    wts(jnp.int32(0), True)(start)
    da[...] = jnp.zeros(da.shape, F32)
    done(ins)
    lane = lax.broadcasted_iota(jnp.int32, (HALF, W), 1)
    events = {
        1: [y0.pass_on, z0.pass_on],
        2: [y1.pass_on, y2.pass_on, y0.share, y0.ready],
        4: [y1.share, y1.ready],
        6: [y2.share, y2.ready],
        9: [z0.share, z0.ready],
    }

    def tile(j, _):
        k = par(j)
        for n_, todo in events.items():
            @pl.when(j == n_)
            def _():
                for f in todo:
                    f()
                wts(j, True)(start)

        @pl.when(j + 1 < TILES)
        def _():
            ahead = j >= 0
            for n_ in events:
                ahead = ahead & (j + 1 != n_)

            @pl.when(ahead)
            def _():
                wts(j + 1, True)(start)
        wts(j, True)(done)

        @pl.when(j >= PAIR)
        def _():
            done(outs(j - PAIR))
        keep = lane >= LANES * (j // LAST)

        def part(r):
            g, u = dot(a[r], wg[k].reshape(D, W)), dot(a[r], wu[k].reshape(D, W))
            d = dot(dy[r], wd[k], NT).astype(BF).astype(F32)
            t, dg, du = hidden(d, g, u)
            actb[k, r] = t.astype(BF)
            dgb[k, r] = jnp.where(keep, dg, 0.0).astype(BF)
            dub[k, r] = jnp.where(keep, du, 0.0).astype(BF)
        halves(part)
        start(outs(j))
        return 0
    lax.fori_loop(0, TILES, tile, 0)
    for j in range(TILES - PAIR, TILES):
        done(outs(j))
    for part in parts:
        part.finish()

    def next_(j):
        start(back(j))
        wts(j, False)(start)
    next_(jnp.int32(0))

    def tile1(j):
        k = par(j)

        @pl.when(j + 1 < TILES)
        def _():
            next_(j + 1)
        done(back(j))
        wts(j, False)(done)

        def part(r):
            for q in range(NX):
                g, u = (w[k, CORES * q:CORES * q + CORES].reshape(W, W) for w in (wg, wu))
                da[q, r] += dot(dgb[k, r], g, NT) + dot(dub[k, r], u, NT)
        halves(part)

    def put1(j):
        sums.gu.free(j, 0)
        sums.put(j, 0, aT[...], dgb[par(j)])
        sums.put(j, 1, aT[...], dub[par(j)])

    def hs(i):
        return fetch(h_h.at[seg(i, ROWS)], hb.at[par(i)], s_h.at[par(i)])
    chunks = T // ROWS
    a0 = fetch(a0T_h, aT, s_in.at[0])

    def norm(i):
        @pl.when(i == 0)
        def _():
            a0.start()
            hs(i).start()

        def chunk(n_, _):
            r = seg(n_, ROWS)

            @pl.when(n_ + 1 < chunks)
            def _():
                hs(n_ + 1).start()
            hs(n_).wait()
            wide, scale = norm_of(hb[par(n_)])
            cut = [slice(W * q, W * q + W) for q in range(NX)]
            along = sum(jnp.sum(da[q, r] * wide[:, cut[q]], -1, keepdims=True) for q in range(NX))
            along = scale * scale * scale * (along / D)
            for q in range(NX):
                t = scale * da[q, r] - wide[:, cut[q]] * along
                dy[r, cut[q]] = (dy[r, cut[q]].astype(F32) + t).astype(BF)
            dyT[:, r] = dy[r].T
            return 0
        each = chunks // NORM_STEPS
        lax.fori_loop(i * each, i * each + each, chunk, 0)

    def tiles(j):
        k = par(j)
        return [fetch(wd0_h.at[tile_cols(j)], wd.at[k], s_w.at[CORES, k]), fetch(g_h.at[j], da.at[CORES * k], s_w.at[0, k]), fetch(u_h.at[j], da.at[CORES * k + 1], s_w.at[1, k])]

    def before0(_):
        a0.wait()
        start(tiles(jnp.int32(0)))

    def tile0(j):
        k = par(j)

        @pl.when(j + 1 < TILES)
        def _():
            start(tiles(j + 1))
        done(tiles(j))

        def part(r):
            d = dot(dy[r], wd[k], NT).astype(BF).astype(F32)
            _, dg, du = hidden(d, da[CORES * k, r], da[CORES * k + 1, r])
            dgb[0, r], dub[0, r] = dg.astype(BF), du.astype(BF)
        halves(part)
        sums.gu.free(TILES + j, 0)
        sums.put(TILES + j, 0, aT[...], dgb[0])

    def put0(j):
        sums.put(TILES + j, 1, aT[...], dub[0])
    sums.loop(tile1, put1, norm, before0, tile0, put0)


def bb(*args):
    tiles = S((TILES, T, W), BF)
    return pl.pallas_call(
        bb_kernel, name="bb",
        out_shape=[S((PAIR, LAYERS, GR, F), BF), S((LAYERS, NY * LANES, D), BF), S((LAYERS, F, D), BF), tiles, tiles, tiles, S((PAIR, SHARDS, GR, F), BF)],
        in_specs=[ANY] * len(args), out_specs=[ANY] * 7,
        scratch_shapes=[V((T, D), BF), V((D, T), BF), V((T, D), BF), V((D, T), BF), V((NX, T, W), F32), slots(GR, F), slots(SHARDS, GR, W), slots(SHARDS, GR, W), slots(W, D),
                        slots(T, W), slots(T, W), slots(T, W), V((W, D), BF), V((NX, DR, W), BF), slots(ROWS, D),
                        DMA((4,)), DMA((2,)), DMA((3, 2)), DMA((3, 2)), DMA((1,)), DMA((NX,)), DMA((2,))]
        + [s for part in bb_parts() for s in part.scratch()] + Sums().scratch(),
        compiler_params=params(2), cost_estimate=cost(12),
    )(*args)[:2]


def adamw(w, m, v, g):
    m = 0.9 * m + 0.1 * g
    v = 0.95 * v + 0.05 * g * g
    step = m * lax.rsqrt(v + 1e-8) + 0.1 * w
    return (w - 0.02 * step).astype(BF), m, v


def solution(mesh):
    def step(x, dy, *arrays):
        weights, m, v = (arrays[i:i + 3] for i in (0, 3, 6))
        x, dy = x[0], dy[0]
        _, d0, d1, head, g0, u0, act0, h1, a1, a1T, a0T, dyT = fa(x, dy, *weights)
        gu, dn = bb(a1, a1T, dy, dyT, h1, weights[0], weights[1], head, d1.reshape(F, D), a0T, act0, g0, u0, d0.reshape(F, D))
        grads = [gu[0], gu[1], dn[:, :DR]]
        new = [adamw(w.astype(F32), m_, v_, g.astype(F32)) for w, m_, v_, g in zip(weights, m, v, grads)]
        return tuple(one[k] for k in range(3) for one in new)

    states, cut = P(("rep", "r", "s"), None, None), P(None, "s", None)
    return jax.shard_map(step, mesh=mesh, in_specs=(states, states) + (cut,) * 9, out_specs=(P("rep", "s", None),) * 9, check_vma=False)
```

time: 899 us -> 491 us (0.55)
  Pallas kernels: 0 us -> 470 us
  waiting for transfers between devices: 452 us -> 0 us
  matrix products: 373 us -> 0 us
  local copies, waits for them, and re-layouts: 26.5 us -> 4.76 us
  between operations: 14.3 us -> 0.71 us
  other arithmetic: 24 us -> 15 us
    pallas_call x0 -> x2, Pallas kernels: none -> 470 us  [the longest x1 353 us: bb(): pl.pallas_call(bb_kernel, name='bb', out_shape=[S((PAIR, LAYERS, GR, F),...]
    dot_general x15 -> x0, matrix products: 373 us -> none  [the longest x5 137 us: layer(): gate = jnp.dot(a, w['w_gate'], preferred_element_type=jnp.float32)]
    psum x1 -> x0, waiting for transfers between devices: 176 us -> none  [summed(): lax.psum(lax.psum_scatter(term, 's', scatter_dimension=0, tiled=True), 'r')]
    all_gather x6 -> x0, waiting for transfers between devices: 139 us -> none  [fetched(): lax.all_gather(w[number], 's', axis=0, tiled=True)]
    reduce_scatter x6 -> x0, waiting for transfers between devices: 136 us -> none  [summed(): lax.psum_scatter(term, 's', scatter_dimension=0, tiled=True)]
    unnamed x42 -> x12, local copies, waits for them, and re-layouts: 19.8 us -> 4.76 us
  transfers between devices with their start and end apart: 13 -> 0, of which waited for: 10 -> 0; matrix products, arithmetic and copies ran while one was open for 33% -> 0% of each run, Pallas kernels for 0% -> 0%
where the time goes in v1:
time: 491 us; the launch traced here: 490 us
  Pallas kernels  470 us (96%)
  other arithmetic  15 us (3%)
    pallas_call x1, Pallas kernels, bb(): pl.pallas_call(bb_kernel, name='bb', out_shape=[S((PAIR, LAYERS, GR, F),...  353 us
    pallas_call x1, Pallas kernels, fa(): pl.pallas_call(fa_kernel, name='fa', out_shape=[S((PAIR, SHARDS, GR, F),...  117 us
    convert_element_type x2, other arithmetic, adamw(): return ((w - 0.02 * step).astype(BF), m, v)  15 us

profile of v1, /device:TPU:2, one launch (start us, length us, event | category | flops | bytes accessed | tf_op | source)
XLA Modules:
  0.0 490.2 jit_solution(17403892668754887071)
XLA Ops:
  0.6 117.0 %fa.1 = (bf16[2,8,128,3200]{3,2,1,0:T(8,128)(2,1)}, bf16[8,400,1024]{2,1,0:T(8,128)(2,1)}, bf16[8,400,1024]{2,1,0:T(8,128)(2,1)}, bf16[2,8,128,512]{3,2,1,0:T(8,...) custom-call(bf16[2048,1024]{1,0:T(8,128)(2,1)} %bitcast.16, ...), custom_call_target="tpu_custom_call" | custom-call | flops 40265318400 | bytes 67043328 | tf_op jit(solution)/shard_map/fa/pallas_call | solution.py:682
  117.6 352.7 %bb.1 = (bf16[2,2,128,3200]{3,2,1,0:T(8,128)(2,1)}, bf16[2,512,1024]{2,1,0:T(8,128)(2,1)}, bf16[2,3200,1024]{2,1,0:T(8,128)(2,1)}, bf16[13,2048,256]{2,1,0:T(8,1...) custom-call(bf16[2048,1024]{1,0:T(8,128)(2,1)} %get-tuple-element.22.ref, ...), custom_call_target="tpu_custom_call" | custom-call | flops 161061273600 | bytes 67043328 | tf_op jit(solution)/shard_map/bb/pallas_call | solution.py:880
  470.3 0.0 copy-start
  470.4 0.0 copy-start.1
  470.4 0.0 copy-start.2
  470.4 0.0 copy-start.3
  470.4 0.0 copy-start.4
  470.4 0.0 copy-start.5
  470.4 7.1 %fusion.8 = (bf16[2,400,1024]{2,1,0:T(8,128)(2,1)}, f32[2,400,1024]{2,1,0:T(8,128)}, f32[2,400,1024]{2,1,0:T(8,128)}) fusion(bf16[2,400,1024]{2,1,0:T(8,128)(2,1)} %refs_4_.1, bf16[2,512,1024]{2,1,0:T(8,128)(2,1)} %get-tuple-element.34, f32[2,400,1024]{2,1,0:T(8,128)} %param.21, f32[2,400,1024]{2,1,0:T(8,128)} %param.18), kind=kLoop, calls=%fused_computation.22 | loop fusion | flops 13107200 | bytes 18022400 | tf_op jit(solution)/shard_map/convert_element_type | solution.py:896
  477.5 0.0 copy-done
  477.5 1.5 copy-done.1
  479.0 0.9 copy-done.2
  480.0 0.9 copy-done.3
  480.9 0.9 copy-done.4
  481.9 0.4 copy-done.5
  482.3 7.9 %fusion.5 = (bf16[2,128,3200]{2,1,0:T(8,128)(2,1)}, f32[2,128,3200]{2,1,0:T(8,128)}, f32[2,128,3200]{2,1,0:T(8,128)}, bf16[2,128,3200]{2,1,0:T(8,128)(2,1)}, f32...) fusion(bf16[2,128,3200]{2,1,0:T(8,128)(2,1)S(1)} %copy-done.5, bf16[2,2,128,3200]{3,2,1,0:T(8,128)(2,1)S(1)} %copy-done.4, ...), kind=kLoop, calls=%fused_computation.19 | loop fusion | flops 26214400 | bytes 36044800 | tf_op jit(solution)/shard_map/convert_element_type | solution.py:896
Async XLA Ops:
  470.3 7.2 %copy-start = (f32[2,128,3200]{2,1,0:T(8,128)S(1)}, f32[2,128,3200]{2,1,0:T(8,128)}, u32[]{:S(2)}) copy-start(f32[2,128,3200]{2,1,0:T(8,128)} %param.20) | copy-start | bytes 9830404
  470.4 8.7 %copy-start.1 = (f32[2,128,3200]{2,1,0:T(8,128)S(1)}, f32[2,128,3200]{2,1,0:T(8,128)}, u32[]{:S(2)}) copy-start(f32[2,128,3200]{2,1,0:T(8,128)} %param.17) | copy-start | bytes 9830404
  470.4 9.6 %copy-start.2 = (f32[2,128,3200]{2,1,0:T(8,128)S(1)}, f32[2,128,3200]{2,1,0:T(8,128)}, u32[]{:S(2)}) copy-start(f32[2,128,3200]{2,1,0:T(8,128)} %param.19) | copy-start | bytes 9830404
  470.4 10.5 %copy-start.3 = (f32[2,128,3200]{2,1,0:T(8,128)S(1)}, f32[2,128,3200]{2,1,0:T(8,128)}, u32[]{:S(2)}) copy-start(f32[2,128,3200]{2,1,0:T(8,128)} %param.16) | copy-start | bytes 9830404
  470.4 11.5 %copy-start.4 = (bf16[2,2,128,3200]{3,2,1,0:T(8,128)(2,1)S(1)}, bf16[2,2,128,3200]{3,2,1,0:T(8,128)(2,1)}, u32[]{:S(2)}) copy-start(bf16[2,2,128,3200]{3,2,1,0:T(8,128)(2,1)} %get-tuple-element.33) | copy-start | bytes 9830404
  470.4 11.9 %copy-start.5 = (bf16[2,128,3200]{2,1,0:T(8,128)(2,1)S(1)}, bf16[2,128,3200]{2,1,0:T(8,128)(2,1)}, u32[]{:S(2)}) copy-start(bf16[2,128,3200]{2,1,0:T(8,128)(2,1)} %refs_6_.1) | copy-start | bytes 4915204

commit v2 on v1

v2 whole, which is shorter than its diff:
```python
import jax
import jax.numpy as jnp
from jax import lax
from jax.experimental import pallas as pl
from jax.experimental.pallas import tpu as pltpu
from jax.sharding import PartitionSpec as P

BF, F32 = jnp.bfloat16, jnp.float32
NN, NT = (((1,), (0,)), ((), ())), (((1,), (1,)), ((), ()))
DMA, V, S = pltpu.SemaphoreType.DMA, pltpu.VMEM, jax.ShapeDtypeStruct
ANY = pl.BlockSpec(memory_space=pl.ANY)
LIMIT = 67_043_328
LAYERS, CORES, NX, NY, NZ = 2, 2, 4, 4, 8
SHARDS = NX * CORES
T, D, F = 2048, 1024, 3200
LANES, W, HALF, GROUP = 128, 256, 1024, 512
TILES = -(-F // W)
LAST = TILES - 1
GR, DR = D // SHARDS, F // SHARDS
PAIR = 2
ROWS, HB = 256, 3


def par(i):
    return lax.rem(i, PAIR)


def seg(i, n, step=None):
    return pl.ds(pl.multiple_of(i * (n if step is None else step), n), n)


def off(j):
    return pl.multiple_of(W * j - (TILES * W - F) * (j // LAST), LANES)


def tile_cols(j):
    return pl.ds(off(j), W)


def dot(a, b, dn=NN):
    return lax.dot_general(a, b, dn, preferred_element_type=F32)


def fetch(src, dst, sem):
    return pltpu.make_async_copy(src, dst, sem)


def start(copies):
    for c in copies:
        c.start()


def done(copies):
    for c in copies:
        c.wait()


def got(copies):
    for c in copies:
        c.wait_recv()


def sent(copies):
    for c in copies:
        c.wait_send()


def norm_of(h):
    wide = h.astype(F32)
    return wide, lax.rsqrt(jnp.mean(wide * wide, -1, keepdims=True) + 1e-6)


class Place:
    def __init__(self):
        r, s = lax.axis_index("r"), lax.axis_index("s")
        self.x, self.c, self.y, self.z = s // CORES, lax.rem(s, CORES), r // NZ, lax.rem(r, NZ)
        self.me = s

    def at(self, x, y, z, c):
        return {"r": y * NZ + z, "s": x * CORES + c}

    def along(self, axis, d):
        if axis == "x":
            return self.at(lax.rem(self.x + d, NX), self.y, self.z, self.c)
        if axis == "y":
            return self.at(self.x, lax.rem(self.y + d, NY), self.z, self.c)
        return self.at(self.x, self.y, lax.rem(self.z + d, NZ), self.c)

    def sib(self):
        return self.at(self.x, self.y, self.z, 1 - self.c)

    def greet(self):
        bar = pltpu.get_barrier_semaphore()
        peers = [self.sib()] + [self.along(a, d) for a, n in SIZES.items() for d in range(1, n)]
        for q in peers:
            pl.semaphore_signal(bar, inc=1, device_id=q, device_id_type=pl.DeviceIdType.MESH)
        pl.semaphore_wait(bar, len(peers))


BOTH = 2
SIZES = {"x": NX, "y": NY, "z": NZ}


def rcopy(src, dst, ss, rs, to):
    return pltpu.make_async_remote_copy(src, dst, ss, rs, device_id=to, device_id_type=pl.DeviceIdType.MESH)


class Gather:
    def __init__(self, route, first, width, rows=None):
        self.route, self.first, self.width, self.gu = route, first, width, rows is None
        self.rows = pl.ds(0, GR) if rows is None else pl.ds(*rows)

    def scratch(self):
        return [DMA((PAIR,))] * 4 + [DMA((1,))]

    def bind(self, p, refs, own, full, base=0):
        self.p, self.own, self.full, self.base = p, own, full, base
        self.a, self.b, self.c, self.o, self.l = refs
        return self

    def whole(self):
        return (self.rows, pl.ds(self.first, self.width))

    def piece(self):
        q, n = (self.p.y, NY) if self.route == "y" else (self.p.z, NZ)
        if self.gu:
            return (seg(q, GR // n), pl.ds(self.first, self.width))
        n = self.width // n
        return (self.rows, pl.ds(pl.multiple_of(self.first + q * n, n), n))

    def mine(self, where):
        if self.base:
            where = (where[0], pl.ds(self.first - self.base, self.width))
        return self.own.at[(slice(None),) + where] if self.gu else self.own.at[where]

    def block(self, s, where):
        return self.full.at[(slice(None), s) + where] if self.gu else self.full.at[(s,) + where]

    def shard(self, k):
        return CORES * lax.rem(self.p.x + k, NX) + self.p.c

    def A(self):
        where = self.whole() if self.route == "x" else self.piece()
        return [rcopy(self.mine(where), self.block(self.p.me, where), self.a.at[0], self.a.at[1], self.p.along("x", d)) for d in range(1, NX)]

    def B(self):
        out, where = [], self.piece()
        for k in range(1, NX):
            b = self.block(self.shard(k), where)
            out += [rcopy(b, b, self.b.at[0], self.b.at[1], self.p.along(self.route, d)) for d in range(1, SIZES[self.route])]
        return out

    def O(self):
        w = self.whole()
        return [rcopy(self.mine(w), self.block(self.p.me, w), self.o.at[0], self.o.at[1], self.p.sib())]

    def C(self):
        out = []
        for k in range(1, NX):
            b = self.block(self.shard(k), self.whole())
            out.append(rcopy(b, b, self.c.at[0], self.c.at[1], self.p.sib()))
        return out

    def all_of(self, sems, where):
        b = self.block(pl.ds(0, NX - 1), where)
        return [rcopy(b, b, sems.at[0], sems.at[1], self.p.sib())]

    def all_A(self):
        return self.all_of(self.a, self.whole() if self.route == "x" else self.piece())

    def all_B(self):
        n = SIZES[self.route]
        if self.gu:
            return self.all_of(self.b, (pl.ds(0, GR // n * (n - 1)), pl.ds(self.first, self.width)))
        return self.all_of(self.b, (self.rows, pl.ds(self.first, self.width // n * (n - 1))))

    def all_C(self):
        return self.all_of(self.c, self.whole())

    def local(self):
        w = self.whole()
        return [fetch(self.mine(w), self.block(self.p.me, w), self.l.at[0])]

    def go(self):
        start(self.A() + self.O() + self.local())

    def pass_on(self):
        got(self.all_A())
        start(self.B())

    def share(self):
        got(self.all_A() if self.route == "x" else self.all_B())
        start(self.C())

    def ready(self):
        got(self.all_C() + self.O())
        done(self.local())

    def finish(self):
        sent(self.all_A() + self.O() + self.all_C() + (self.all_B() if self.route != "x" else []))


HEAD = 3 * W


def fa_parts():
    gu = [Gather(*a) for a in (("x", 0, W), ("x", W, W), ("y", 512, 512), ("y", 1024, 512), ("y", 1536, 512), ("x", 2048, W), ("z", 2304, 896))]
    d0 = [Gather(r, f, GROUP, (0, DR)) for r, f in (("x", 0), ("y", GROUP))]
    d1 = [Gather("z", 0, D, (0, 208)), Gather("y", 0, D, (208, 192))]
    return gu, d0, d1, [Gather("x", 0, HEAD)]


def bb_parts():
    return [Gather(*a) for a in (("y", HEAD, 512), ("x", 1280, 512), ("y", 1792, 512), ("z", 2304, 896))]


FRESH0, FRESH1 = (0, 1, 9), (3, 9)


def refs_of(parts, refs):
    n = len(parts[0].scratch())
    return [refs[n * i:n * i + n] for i in range(len(parts))]


class Engine:
    def __init__(self, gu, ring):
        self.gu, self.ring, self.routes = gu, ring, ("x", "y") if gu else ("x", "x")
        self.R, self.C = (GR, W) if gu else (DR, LANES)
        self.P = 32 if gu else LANES
        self.zr = self.P // (PAIR if gu else NX)
        self.lo = self.R // PAIR if gu else 208

    def scratch(self):
        R, C, Q, n = self.R, self.C, self.P, self.ring
        half = (PAIR, NX, R, C) if self.gu else (NX, R, PAIR * C)
        first = [V((n, PAIR, R, C) if r == "x" else (n, PAIR, NX, Q, C), BF) for r in self.routes]
        relay = [V((n, PAIR, self.lo, C) if r == "x" else (n, PAIR, PAIR, Q, C), BF) for r in self.routes]
        then = [V((PAIR, NY * Q, C) if r == "x" else (PAIR, NX, Q, C), BF) for r in self.routes]
        part = (NZ, self.zr, LANES)
        sems = [(PAIR,), (n,), (PAIR, PAIR), (n, PAIR), (PAIR, PAIR), (n, PAIR)] + [(PAIR,), (n,)] * 5
        return ([V((n,) + half, BF), V((n, PAIR, NX, R, C), BF)] + relay + first + then
                + [V((n, PAIR, NX - 1, Q, C), BF), V((PAIR,) + part, BF), V((n,) + part, BF), V((n,) + part, BF)]
                + [V((PAIR, PAIR, Q, C) if self.gu else (PAIR, Q, PAIR * C), BF)]
                + [DMA(s) for s in sems + [(PAIR,)]])

    REFS = 30

    def bind(self, p, refs, own, src, out_at):
        self.p, self.own, self.src, self.out_at = p, own, src, out_at
        (self.rS, self.XS, la, lb, a, b, ya, yb, self.R2, self.Zp, self.R3, self.ZG, self.YS, self.s0, self.r0, self.s1, self.r1,
         self.s2, self.r2, self.s3, self.r3, self.s4, self.r4, self.s5, self.r5, self.s6, self.r6, self.s7, self.r7, self.so) = refs
        self.RL, self.R1, self.Y = (la, lb), (a, b), (ya, yb)
        if not self.gu:
            for y in self.Y:
                for k in range(PAIR):
                    y[k, DR:] = jnp.zeros((NY * self.P - DR, self.C), BF)

    def slot(self, it):
        return lax.rem(it, self.ring)

    def c0(self, it):
        k, n_, n = par(it), self.slot(it), (1 if self.gu else NX)
        return [rcopy(self.src(it, i), self.rS.at[n_] if self.gu else self.rS.at[n_, i], self.s0.at[k], self.r0.at[n_], self.p.sib()) for i in range(n)]

    def ypart(self, y):
        return seg(y, self.P)

    def around(self, m):
        q = self.p.x if self.routes[m] == "x" else self.p.y
        return q, ((1, lax.rem(q + 1, NX)), (NX - 1, lax.rem(q + NX - 1, NX)))

    def half(self, it, m, q, i):
        n, R, lo = self.slot(it), self.R, self.lo
        if self.routes[m] == "x":
            return (n, m, q, (slice(0, lo), slice(lo, R))[i])
        return (n, m, slice(PAIR * i, PAIR * i + PAIR), self.ypart(q))

    def relayed(self, it, m, i):
        r = self.RL[m].at[self.slot(it), i]
        return r.at[pl.ds(0, (self.lo, self.R - self.lo)[i])] if self.routes[m] == "x" else r

    def c1(self, it):
        k, n, out = par(it), self.slot(it), []
        for m, route in enumerate(self.routes):
            q, near = self.around(m)
            for i, (d, _) in enumerate(near):
                out.append(rcopy(self.XS.at[self.half(it, m, lax.rem(q + CORES, NX), i)], self.relayed(it, m, i), self.s1.at[k, m], self.r1.at[n, m], self.p.along(route, d)))
        return out

    def c2(self, it):
        k, n, out = par(it), self.slot(it), []
        for m, route in enumerate(self.routes):
            for i, (d, q) in enumerate(self.around(m)[1]):
                src = self.XS.at[n, m, q] if route == "x" else self.XS.at[n, m, :, self.ypart(q)]
                out.append(rcopy(src, self.R1[m].at[n, i], self.s2.at[k, m], self.r2.at[n, m], self.p.along(route, d)))
        return out

    def c3(self, it):
        k, n, p, out = par(it), self.slot(it), self.p, []
        for d in range(1, NX):
            for m, route in enumerate(self.routes):
                src = self.Y[m].at[k, self.ypart(lax.rem(p.y + d, NY))] if route == "x" else self.Y[m].at[k, lax.rem(p.x + d, NX)]
                out.append(rcopy(src, self.R2.at[n, m, d - 1], self.s3.at[k], self.r3.at[n], p.along("y" if route == "x" else "x", d)))
        return out

    def c4(self, it):
        k, n, p = par(it), self.slot(it), self.p
        return [rcopy(self.Zp.at[k, lax.rem(p.z + d, NZ)], self.R3.at[n, d], self.s4.at[k], self.r4.at[n], p.along("z", d)) for d in range(1, NZ)]

    def c5(self, it):
        k, n, p = par(it), self.slot(it), self.p
        b = self.ZG.at[n, p.z]
        return [rcopy(b, b, self.s5.at[k], self.r5.at[n], p.along("z", d)) for d in range(1, NZ)]

    def c6(self, it, src, dst):
        k, n = par(it), self.slot(it)
        b = dst(self.p.y, None)
        return [rcopy(src, b, self.s6.at[k], self.r6.at[n], self.p.along("y", d)) for i, d in enumerate((1, NY - 1))]

    def c7(self, it, src, dst):
        k, n, out = par(it), self.slot(it), []
        for i, d in enumerate((1, NY - 1)):
            b = dst(lax.rem(self.p.y + NY - d, NY), i)
            out.append(rcopy(b, b, self.s7.at[k], self.r7.at[n], self.p.along("y", d)))
        return out

    def whole(self, it, k, dst=None):
        i, n = par(it), self.slot(it)

        def of(ref, ss, rs):
            return rcopy(ref, ref, ss, rs, self.p.sib())
        if k == 0:
            return [of(self.rS.at[n], self.s0.at[i], self.r0.at[n])]
        if k == 1:
            return [of(self.XS.at[n, m, 0] if r == "x" else self.RL[m].at[n], self.s1.at[i, m], self.r1.at[n, m]) for m, r in enumerate(self.routes)]
        if k == 2:
            return [of(self.R1[m].at[n], self.s2.at[i, m], self.r2.at[n, m]) for m in range(PAIR)]
        ref = {3: self.R2.at[n], 4: self.R3.at[n, pl.ds(1, NZ - 1)], 5: self.ZG.at[n, pl.ds(1, NZ - 1)], 6: dst and dst(0, BOTH), 7: dst and dst(self.p.y, None)}[k]
        ss, rs = {3: (self.s3, self.r3), 4: (self.s4, self.r4), 5: (self.s5, self.r5), 6: (self.s6, self.r6), 7: (self.s7, self.r7)}[k]
        return [of(ref, ss.at[i], rs.at[n])]

    def out(self, it, f):
        for cond, src, dst in self.out_at(it):
            @pl.when(cond)
            def _():
                f(src, dst)

    def left(self, it, k):
        if k < 6:
            return sent(self.whole(it, k))

        def f(src, dst):
            sent(self.whole(it, k, dst))
            if k == 6:
                fetch(src, dst(self.p.y, None), self.so.at[par(it)]).wait()
        self.out(it, f)

    def free(self, it, k):
        @pl.when(it >= PAIR)
        def _():
            self.left(it - PAIR, k)

    def S0(self, it):
        start(self.c0(it))

    def S1(self, it):
        k, n, C = par(it), self.slot(it), self.C
        got(self.whole(it, 0))
        self.free(it, 1)

        def add(xx, _):
            for m in range(PAIR):
                other = self.rS[n, m, xx] if self.gu else self.rS[n, xx, :, m * C:m * C + C]
                self.XS[n, m, xx] = (self.own(it, m, xx).astype(F32) + other.astype(F32)).astype(BF)
            return 0
        lax.fori_loop(0, NX, add, 0)
        start(self.c1(it))

    def S2(self, it):
        got(self.whole(it, 1))
        self.free(it, 2)
        for m, route in enumerate(self.routes):
            for i, (_, q) in enumerate(self.around(m)[1]):
                w, r = self.half(it, m, q, i), self.relayed(it, m, i)
                self.XS[w] = (self.XS[w].astype(F32) + r[...].astype(F32)).astype(BF)
        start(self.c2(it))

    def S3(self, it):
        k, n, p = par(it), self.slot(it), self.p
        got(self.whole(it, 2))
        self.free(it, 3)
        for m, route in enumerate(self.routes):
            t = (self.XS[n, m, p.x] if route == "x" else self.XS[n, m, :, self.ypart(p.y)]).astype(F32)
            for i in range(PAIR):
                t = t + self.R1[m][n, i].astype(F32)
            if route == "x":
                self.Y[m][k, :self.R] = t.astype(BF)
            else:
                self.Y[m][k] = t.astype(BF)
        start(self.c3(it))

    def S4(self, it):
        k, n, p = par(it), self.slot(it), self.p
        got(self.whole(it, 3))
        self.free(it, 4)
        for m, route in enumerate(self.routes):
            t = (self.Y[m][k, self.ypart(p.y)] if route == "x" else self.Y[m][k, p.x]).astype(F32)
            for d in range(NY - 1):
                t = t + self.R2[n, m, d].astype(F32)
            t = t.astype(BF)
            for q in range(NX):
                self.Zp[k, m * NX + q] = t[self.quarter(q)]
        start(self.c4(it))

    def quarter(self, q):
        z = self.zr
        if not self.gu:
            return (slice(z * q, z * q + z), slice(None))
        a, b = z * (q // PAIR), LANES * (q % PAIR)
        return (slice(a, a + z), slice(b, b + LANES))

    def S5(self, it):
        k, n, p = par(it), self.slot(it), self.p
        got(self.whole(it, 4))
        self.free(it, 5)
        t = self.Zp[k, p.z].astype(F32)
        for d in range(1, NZ):
            t = t + self.R3[n, d].astype(F32)
        self.ZG[n, p.z] = t.astype(BF)
        start(self.c5(it))

    def S6(self, it):
        k, n = par(it), self.slot(it)
        got(self.whole(it, 5))
        self.free(it, 6)
        for q in range(NZ):
            m, (a, b) = q // NX, self.quarter(q % NX)
            if self.gu:
                self.YS[k, m, a, b] = self.ZG[n, q]
            else:
                self.YS[k, a, m * LANES:m * LANES + LANES] = self.ZG[n, q]

        def f(src, dst):
            start(self.c6(it, src, dst) + [fetch(src, dst(self.p.y, None), self.so.at[k])])
        self.out(it, f)

    def S7(self, it):
        self.free(it, 7)

        def f(src, dst):
            got(self.whole(it, 6, dst))
            start(self.c7(it, src, dst))
        self.out(it, f)

    def S8(self, it):
        self.out(it, lambda src, dst: got(self.whole(it, 7, dst)))

    def stage(self, k, there, it):
        @pl.when(there)
        def _():
            (self.S0, self.S1, self.S2, self.S3, self.S4, self.S5, self.S6, self.S7, self.S8)[k](it)

    def finish(self, items):
        for it in range(items - PAIR, items):
            for k in range(8):
                self.left(jnp.int32(it), k)


OFFS = (0, 2, 4, 6, 8, 10, 12, 14, 16)
LATER = (8, 7, 6, 5, 4, 3, 2)
WIDE_STEPS = 4
AT_DOWN1 = TILES
AT_DOWN0 = AT_DOWN1 + WIDE_STEPS
AT_TILES0 = AT_DOWN0 + WIDE_STEPS
STEPS = AT_TILES0 + TILES + OFFS[-1]
DN_STRIDE, DN_EACH = 3, D // W
DN_ITEMS = LAYERS * DN_EACH


def gu_item(u):
    v = lax.max(u, 0)
    return ((u >= 0) & (v < TILES)) | ((v >= AT_TILES0) & (v < AT_TILES0 + TILES)), v - (AT_TILES0 - TILES) * (v // AT_TILES0)


def dn_item(u):
    v = lax.max(u - AT_DOWN0, 0)
    w = v - DN_EACH
    there = (v < DN_EACH) | ((lax.rem(v, DN_STRIDE) == 0) & (w < DN_STRIDE * DN_EACH))
    return (u >= AT_DOWN0) & there, lax.min(v, DN_EACH) + lax.max(w, 0) // DN_STRIDE


class Down:
    def __init__(self, p, act_hs, dhTs, h, ab, buf, town, s_a, s_o, s_t):
        self.p, self.act_hs, self.dhTs, self.h, self.ab, self.buf, self.town = p, act_hs, dhTs, h, ab, buf, town
        self.s_a, self.s_o, self.s_t = s_a, s_o, s_t

    def run(self, n, i, loads=None, work=None):
        def store(q, k):
            return fetch(self.buf.at[k], self.h.at[n, tile_cols(q)], self.s_o.at[k])

        def run(pairs, ab, other, nxt):
            q = PAIR * nxt - PAIR
            self.load(n, q, ab).wait()

            @pl.when(nxt <= LAST // PAIR)
            def _():
                self.load(n, PAIR * nxt, other).start()

            @pl.when(q > 0)
            def _():
                for k in range(PAIR):
                    store(q - PAIR + k, k).wait()
            chunks = [nxt - 1] + ([nxt] if pairs < PAIR else [])
            if work:
                loads(chunks)
            for k in range(pairs):
                self.buf[k] = dot(self.dhTs[n][...], ab[k + PAIR - pairs]).astype(BF).T
            if work:
                for c in chunks:
                    work(c)
            for k in range(pairs):
                store(q + k, k).start()

        @pl.when(i < LAST // CORES // CORES)
        def _():
            run(PAIR, self.ab[0], self.ab[1], PAIR * i + 1)
            run(PAIR, self.ab[1], self.ab[0], PAIR * i + 2)

        @pl.when(i == LAST // CORES // CORES)
        def _():
            run(1, self.ab[0], self.ab[1], PAIR * i + 1)
            store(LAST, 0).wait()

    def load(self, n, q, ab):
        return fetch(self.act_hs[n].at[pl.ds(q - q // LAST, PAIR)], ab, self.s_a.at[0])

    def first(self, n):
        self.load(n, jnp.int32(0), self.ab[0]).start()

    def block(self, it, k, c):
        return self.h.at[it // DN_EACH, pl.ds(pl.multiple_of(DR * (CORES * k + c), 16), DR), seg(lax.rem(it, DN_EACH), W)]

    def src(self, it, k):
        return self.block(it, k, 1 - self.p.c)

    def mine(self, it):
        return [fetch(self.block(it, k, self.p.c), self.town.at[par(it), k], self.s_t.at[par(it)]) for k in range(NX)]

    def own(self, it, m, xx):
        return self.town[par(it), xx, :, m * LANES:m * LANES + LANES]

    def hook(self, eng, i):
        for k in LATER:
            eng.stage(k, *dn_item(i - OFFS[k]))
        there, it = dn_item(i - OFFS[1])

        @pl.when(there)
        def _():
            fetch(eng.rS.at[0], self.town.at[0], self.s_t.at[par(it)]).wait()
            eng.S1(it)
        there0, it0 = dn_item(i)

        @pl.when(there0)
        def _():
            eng.free(it0, 0)
            start(self.mine(it0))
            eng.S0(it0)


TERMS = 3


class Sums:
    def __init__(self):
        self.gu, self.dn = Engine(True, 4), Engine(False, 4)

    def scratch(self):
        return [V((TERMS, PAIR, NX, CORES, GR, W), BF)] + self.gu.scratch() + self.dn.scratch()

    def bind(self, p, refs, gu_h, dn_h, down):
        n = Engine.REFS
        self.t, self.down = refs[0], down

        def gu_out(it):
            l, j, e = 1 - it // TILES, lax.rem(it, TILES), self.gu.YS.at[par(it)]

            def to(cols):
                def at(y, half):
                    if half == BOTH:
                        return gu_h.at[:, l, pl.ds(0, 64), cols]
                    return gu_h.at[pl.ds(0, CORES) if half is None else pl.ds(half, 1), l, seg(y, 32), cols]
                return at
            return [(j < LAST, e, to(seg(j, W))), (j == LAST, e.at[:, :, LANES:], to(pl.ds(F - LANES, LANES)))]

        def dn_out(it):
            def to(y, half):
                if half == BOTH:
                    r = pl.ds(0, CORES * LANES)
                else:
                    r = seg(y, LANES) if half is None else seg(CORES * y + half, LANES // CORES)
                return dn_h.at[1 - it // DN_EACH, r, seg(lax.rem(it, DN_EACH), W)]
            return [(it >= 0, self.dn.YS.at[par(it)], to)]
        self.gu.bind(p, refs[1:1 + n], lambda it, m, xx: self.t[lax.rem(it, TERMS), m, xx, p.c], lambda it, k: self.t.at[lax.rem(it, TERMS), :, :, 1 - p.c], gu_out)
        self.dn.bind(p, refs[1 + n:], down.own, down.src, dn_out)

    def put(self, it, m, aT, t):
        self.t[lax.rem(it, TERMS), m] = dot(aT, t).astype(BF).reshape(NX, CORES, GR, W)

    def loop(self, tile1, beside, after1, before0, tile0):
        def when(i, first, n, f):
            @pl.when((i >= first) & (i < first + n))
            def _():
                f(i - first)

        def step(i, _):
            for k in LATER + (1,):
                self.gu.stage(k, *gu_item(i - OFFS[k]))
            self.down.hook(self.dn, i)
            when(i, AT_DOWN1, WIDE_STEPS, lambda j: self.down.run(0, j, *beside))
            when(i, AT_DOWN1 - 1, 1, lambda _: self.down.first(0))
            when(i, AT_DOWN0, 1, lambda _: self.down.first(1))
            when(i, AT_DOWN0, 1, after1)
            when(i, AT_TILES0 - 1, 1, before0)
            when(i, AT_DOWN0, WIDE_STEPS, lambda j: self.down.run(1, j))
            when(i, 0, TILES, tile1)
            when(i, AT_TILES0, TILES, tile0)
            self.gu.stage(0, *gu_item(i))
            return 0
        lax.fori_loop(0, STEPS, step, 0)
        self.gu.finish(LAYERS * TILES)
        self.dn.finish(DN_ITEMS)


def sigmoid(g):
    return 0.5 * jnp.tanh(0.5 * g) + 0.5


def hidden(d, g, u):
    sg = sigmoid(g)
    si = g * sg
    return si * u, d * u * (sg + si * (1 - sg)), d * si


def halves(part):
    lax.fori_loop(0, T // HALF, lambda i, _: (part(seg(i, HALF)), 0)[1], 0, unroll=True)


def stream(n, load, store, work):
    start(load(0))

    def step(i, _):
        @pl.when(i + 1 < n)
        def _():
            start(load(i + 1))
        done(load(i))

        @pl.when(i >= PAIR)
        def _():
            done(store(i - PAIR))
        work(i)
        start(store(i))
        return 0
    lax.fori_loop(0, n, step, 0)
    for i in range(n - PAIR, n):
        done(store(i))


def fa_kernel(*refs):
    (x_h, dy_h, wg_h, wu_h, wd_h, gu0_h, d0_h, d1_h, head_h, g_h, u_h, act_h, h1_h, a1_h, a1T_h, a0T_h, dyT_h,
     own0, own1, ownd, a, wd, act, wg, wu, gb, ub, xb, hb, ab, atb, s_own, s_w, s_b, s_act, s_x, s_o, s_wd, s_dy), rest = refs[:39], refs[39:]
    p = Place()
    groups = fa_parts()
    every = [part for g in groups for part in g]
    for part, r, (own, full) in zip(every, refs_of(every, rest), [(own0, gu0_h)] * len(groups[0]) + [(ownd.at[0], d0_h)] * 2 + [(ownd.at[1], d1_h)] * 2 + [(own1, head_h)]):
        part.bind(p, r, own, full)
    (x0, x1, y0, y1, y2, x2, z0), (d0x, d0y), (d1z, d1y), (head,) = groups
    owns = [fetch(w.at[0], own0.at[k], s_own.at[k, 0]) for k, w in enumerate((wg_h, wu_h))]
    owns += [fetch(w.at[1, :, pl.ds(0, HEAD)], own1.at[k], s_own.at[k, 1]) for k, w in enumerate((wg_h, wu_h))]
    owns += [fetch(wd_h.at[k], ownd.at[k], s_own.at[CORES, k]) for k in range(LAYERS)]
    start(owns)
    p.greet()
    done(owns)
    for part in (y0, z0, x0, y1, x1, y2, x2, d0y, d1z, d1y, d0x, head):
        part.go()
    n = T // GROUP

    def cut(i):
        return seg(i, GROUP)

    def first(i):
        wide, scale = norm_of(xb[par(i)])
        t = (wide * scale).astype(BF)
        a[cut(i)] = t
        atb[par(i)] = t.T

    def dys(i):
        return fetch(dy_h.at[seg(i, GROUP)], hb.at[i % PAIR], s_dy.at[i % PAIR])

    def turn(i):
        def f():
            dys(i).wait()
            if i >= PAIR:
                turned(dyT_h)(i - PAIR)[0].wait()
            atb[i % PAIR] = hb[i % PAIR].T
            start(turned(dyT_h)(i))
            if i + PAIR < n:
                dys(i + PAIR).start()
        return f

    def load(h):
        return lambda i: [fetch(h.at[cut(i)], xb.at[par(i)], s_x.at[par(i)])]

    def turned(h):
        return lambda i: [fetch(atb.at[par(i)], h.at[:, cut(i)], s_o.at[CORES, par(i)])]
    for i in range(PAIR):
        dys(i).start()
    stream(n, load(x_h), turned(a0T_h), first)

    def wts(j):
        return [fetch(gu0_h.at[k, :, :, tile_cols(j)], w.at[par(j)], s_w.at[k, par(j)]) for k, w in enumerate((wg, wu))]

    def outs(j):
        return [fetch(b.at[par(j)], h.at[j], s_b.at[k, par(j)]) for k, (b, h) in enumerate(((gb, g_h), (ub, u_h)))]

    events = {
        0: [y0.pass_on, z0.pass_on, turn(0), turn(1), x0.share, x0.ready, y1.pass_on],
        1: [turn(2), y0.share, x1.share, x1.ready, y2.pass_on, y0.ready],
        2: [y1.share],
        3: [d0y.pass_on, y1.ready],
        4: [d1z.pass_on, d1y.pass_on, y2.share],
        5: [turn(3), x2.share, y2.ready],
        7: [x2.ready],
        8: [z0.share],
        9: [d0x.share, d0y.share, z0.ready],
        11: [d0x.ready, d0y.ready],
    }

    def tile(j, _):
        k = par(j)
        for n_, todo in events.items():
            @pl.when(j == n_)
            def _():
                for f in todo:
                    f()
                if n_ in FRESH0:
                    start(wts(j))

        @pl.when(j + 1 < TILES)
        def _():
            ahead = j >= 0
            for n_ in FRESH0:
                ahead = ahead & (j + 1 != n_)

            @pl.when(ahead)
            def _():
                start(wts(j + 1))
        done(wts(j))

        @pl.when(j == LAST - 1)
        def _():
            start(wds)

        @pl.when(j >= PAIR)
        def _():
            done(outs(j - PAIR))

        def part(r):
            g, u = dot(a[r], wg[k].reshape(D, W)), dot(a[r], wu[k].reshape(D, W))
            gb[k, r], ub[k, r] = g, u
            act[j, r] = (g * sigmoid(g) * u).astype(BF)
        halves(part)
        start(outs(j) + [fetch(act.at[j], act_h.at[j], s_act.at[j])])
        return 0
    wds = [fetch(d0_h.at[k], wd.at[pl.ds(DR * k, DR)], s_wd.at[k]) for k in range(SHARDS)]
    lax.fori_loop(0, TILES, tile, 0)
    for j in range(TILES - PAIR, TILES):
        done(outs(j))
    for i in range(n - PAIR, n):
        done(turned(dyT_h)(i))
    done(wds)

    def down(i):
        k, r = par(i), cut(i)

        @pl.when(i == 0)
        def _():
            d1y.share()

        @pl.when(i == 1)
        def _():
            d1z.share()
            head.share()
        t = dot(act[LAST, r, LANES:], wd[F - LANES:])
        for j in range(LAST):
            t = t + dot(act[j, r], wd[W * j:W * j + W])
        h = xb[k] + t.astype(BF)
        wide, scale = norm_of(h)
        t = (wide * scale).astype(BF)
        hb[k], ab[k], atb[k] = h, t, t.T

    def finals(i):
        k, r = par(i), cut(i)
        return [fetch(hb.at[k], h1_h.at[r], s_o.at[0, k]), fetch(ab.at[k], a1_h.at[r], s_o.at[1, k]), fetch(atb.at[k], a1T_h.at[:, r], s_o.at[CORES, k])]
    stream(n, load(x_h), finals, down)
    done([fetch(act.at[j], act_h.at[j], s_act.at[j]) for j in range(TILES)])
    for part in (d1z, d1y, head):
        part.ready()
    for part in every:
        part.finish()


def params(number):
    return pltpu.CompilerParams(vmem_limit_bytes=LIMIT, collective_id=number, has_side_effects=True)


def cost(units):
    return pl.CostEstimate(flops=PAIR * units * T * D * F, bytes_accessed=LIMIT, transcendentals=T * F)


def slots(*shape, dtype=BF):
    return V((PAIR,) + shape, dtype)


def fa(x, dy, wg, wu, wd):
    tiles = lambda t: S((TILES, T, W), t)
    full = S((SHARDS, DR, D), BF)
    parts = [part for g in fa_parts() for part in g]
    return pl.pallas_call(
        fa_kernel, name="fa",
        out_shape=[S((PAIR, SHARDS, GR, F), BF), full, full, S((PAIR, SHARDS, GR, HEAD), BF), tiles(F32), tiles(F32), tiles(BF),
                   S((T, D), BF), S((T, D), BF), S((D, T), BF), S((D, T), BF), S((D, T), BF)],
        in_specs=[ANY] * 5, out_specs=[ANY] * 12,
        scratch_shapes=[slots(GR, F), slots(GR, HEAD), slots(DR, D), V((T, D), BF), V((F, D), BF), V((TILES, T, W), BF), slots(SHARDS, GR, W), slots(SHARDS, GR, W),
                        slots(T, W, dtype=F32), slots(T, W, dtype=F32), slots(GROUP, D), slots(GROUP, D), slots(GROUP, D), slots(D, GROUP),
                        DMA((3, 2)), DMA((2, 2)), DMA((2, 2)), DMA((TILES,)), DMA((2,)), DMA((3, 2)), DMA((SHARDS,)), DMA((2,))] + [s for part in parts for s in part.scratch()],
        compiler_params=params(1), cost_estimate=cost(3),
    )(x, dy, wg, wu, wd)


def bb_kernel(*refs):
    (a_h, aT_h, dy_h, dyT_h, h_h, wg_h, wu_h, head_h, wd_h, a0T_h, act0_h, g_h, u_h, wd0_h, gu_h, dn_h, part_h, act_h, dg_h, du_h, w_h,
     a, aT, dy, dyT, da, own, wg, wu, wd, actb, dgb, dub, stage, town, hb, s_in, s_own, s_w, s_b, s_st, s_t, s_h), rest = refs[:43], refs[43:]
    p = Place()
    parts = bb_parts()
    n = sum(len(part.scratch()) for part in parts)
    for part, r in zip(parts, refs_of(parts, rest[:n])):
        part.bind(p, r, own, w_h, HEAD)
    y0, x1, y2, z0 = parts
    down = Down(p, (act_h, act0_h), (dyT, aT), part_h, (actb, dgb), stage, town, s_b.at[0], s_st, s_t)
    sums = Sums()
    sums.bind(p, rest[n:], gu_h, dn_h, down)
    owns = [fetch(w.at[1, :, pl.ds(HEAD, F - HEAD)], own.at[k], s_own.at[k]) for k, w in enumerate((wg_h, wu_h))]
    ins = [fetch(h, v, s_in.at[k]) for k, (h, v) in enumerate(((a_h, a), (dy_h, dy), (aT_h, aT), (dyT_h, dyT)))]

    def wts(j, third):
        def of(w):
            return [fetch(w.at[k, :, :, tile_cols(j)], v.at[par(j)], s_w.at[k, par(j)]) for k, v in enumerate((wg, wu))]

        def both(f):
            @pl.when(j < HEAD // W)
            def _():
                f(of(head_h))

            @pl.when(j >= HEAD // W)
            def _():
                f(of(w_h))
            if third:
                f([fetch(wd_h.at[tile_cols(j)], wd.at[par(j)], s_w.at[CORES, par(j)])])
        return both
    bufs = ((actb, act_h), (dgb, dg_h), (dub, du_h))

    def outs(j):
        return [fetch(b.at[par(j)], h.at[j], s_b.at[k, par(j)]) for k, (b, h) in enumerate(bufs)]

    def back(j):
        return [fetch(h.at[j], b.at[par(j)], s_b.at[k, par(j)]) for k, (b, h) in enumerate(bufs) if k]
    start(owns + ins[:PAIR])
    wts(jnp.int32(0), True)(start)
    start(ins[PAIR:])
    da[...] = jnp.zeros(da.shape, F32)
    p.greet()
    done(owns)
    for part in (y0, z0, y2, x1):
        part.go()
    done(ins[:PAIR])
    lane = lax.broadcasted_iota(jnp.int32, (HALF, W), 1)
    events = {
        1: [y0.pass_on, z0.pass_on],
        2: [y2.pass_on],
        3: [y0.share, y0.ready],
        4: [x1.share, x1.ready],
        5: [y2.share],
        6: [y2.ready],
        8: [z0.share],
        9: [z0.ready],
    }

    def tile(j, _):
        k = par(j)
        for n_, todo in events.items():
            @pl.when(j == n_)
            def _():
                for f in todo:
                    f()
                if n_ in FRESH1:
                    wts(j, True)(start)

        @pl.when(j + 1 < TILES)
        def _():
            ahead = j >= 0
            for n_ in FRESH1:
                ahead = ahead & (j + 1 != n_)

            @pl.when(ahead)
            def _():
                wts(j + 1, True)(start)
        wts(j, True)(done)

        @pl.when(j >= PAIR)
        def _():
            done(outs(j - PAIR))
        keep = lane >= LANES * (j // LAST)

        def part(r):
            g, u = dot(a[r], wg[k].reshape(D, W)), dot(a[r], wu[k].reshape(D, W))
            d = dot(dy[r], wd[k], NT).astype(BF).astype(F32)
            t, dg, du = hidden(d, g, u)
            actb[k, r] = t.astype(BF)
            dgb[k, r] = jnp.where(keep, dg, 0.0).astype(BF)
            dub[k, r] = jnp.where(keep, du, 0.0).astype(BF)
        halves(part)
        start(outs(j))
        return 0
    lax.fori_loop(0, TILES, tile, 0)
    for j in range(TILES - PAIR, TILES):
        done(outs(j))
    done(ins[PAIR:])
    for part in parts:
        part.finish()

    def next_(j):
        start(back(j))
        wts(j, False)(start)
    next_(jnp.int32(0))
    for i in range(PAIR):
        fetch(h_h.at[seg(i, ROWS)], hb.at[i], s_h.at[i]).start()

    def tile1(j):
        k = par(j)

        @pl.when(j + 1 < TILES)
        def _():
            next_(j + 1)
        done(back(j))
        wts(j, False)(done)

        def part(r):
            for q in range(NX):
                g, u = (w[k, CORES * q:CORES * q + CORES].reshape(W, W) for w in (wg, wu))
                da[q, r] += dot(dgb[k, r], g, NT) + dot(dub[k, r], u, NT)
        sums.gu.free(j, 0)
        halves(part)
        sums.put(j, 0, aT[...], dgb[par(j)])
        sums.put(j, 1, aT[...], dub[par(j)])

    def hs(i):
        return fetch(h_h.at[seg(i, ROWS)], hb.at[lax.rem(i, HB)], s_h.at[lax.rem(i, HB)])

    def norm_loads(todo):
        for i in todo:
            hs(i).wait()
        for i in todo:
            @pl.when(i + PAIR < T // ROWS)
            def _():
                hs(i + PAIR).start()

    def norm(i):
        r, k = seg(i, ROWS), lax.rem(i, HB)
        wide, scale = norm_of(hb[k])
        cut = [slice(W * q, W * q + W) for q in range(NX)]
        along = sum(jnp.sum(da[q, r] * wide[:, cut[q]], -1, keepdims=True) for q in range(NX))
        along = scale * scale * scale * (along / D)
        parts = [(dy[r, cut[q]].astype(F32) + (scale * da[q, r] - wide[:, cut[q]] * along)).astype(BF) for q in range(NX)]
        for q in range(NX):
            a[r, cut[q]] = parts[q]
            aT[cut[q], r] = parts[q].T
    a0 = fetch(a0T_h, dyT, s_in.at[0])

    def after1(_):
        a0.start()

    def tiles(j):
        k = par(j)
        return [fetch(wd0_h.at[tile_cols(j)], wd.at[k], s_w.at[CORES, k]), fetch(g_h.at[j], da.at[CORES * k], s_w.at[0, k]), fetch(u_h.at[j], da.at[CORES * k + 1], s_w.at[1, k])]

    def before0(_):
        a0.wait()
        start(tiles(jnp.int32(0)))

    def tile0(j):
        k = par(j)

        @pl.when(j + 1 < TILES)
        def _():
            start(tiles(j + 1))
        done(tiles(j))

        def part(r):
            d = dot(a[r], wd[k], NT).astype(BF).astype(F32)
            _, dg, du = hidden(d, da[CORES * k, r], da[CORES * k + 1, r])
            dgb[0, r], dub[0, r] = dg.astype(BF), du.astype(BF)
        sums.gu.free(TILES + j, 0)
        halves(part)
        sums.put(TILES + j, 0, dyT[...], dgb[0])
        sums.put(TILES + j, 1, dyT[...], dub[0])
    sums.loop(tile1, (norm_loads, norm), after1, before0, tile0)


def bb(*args):
    tiles = S((TILES, T, W), BF)
    return pl.pallas_call(
        bb_kernel, name="bb",
        out_shape=[S((PAIR, LAYERS, GR, F), BF), S((LAYERS, NY * LANES, D), BF), S((LAYERS, F, D), BF), tiles, tiles, tiles, S((PAIR, SHARDS, GR, F), BF)],
        in_specs=[ANY] * len(args), out_specs=[ANY] * 7,
        scratch_shapes=[V((T, D), BF), V((D, T), BF), V((T, D), BF), V((D, T), BF), V((NX, T, W), F32), slots(GR, F - HEAD), slots(SHARDS, GR, W), slots(SHARDS, GR, W), slots(W, D),
                        slots(T, W), slots(T, W), slots(T, W), slots(W, D), slots(NX, DR, W), V((HB, ROWS, D), BF),
                        DMA((4,)), DMA((2,)), DMA((3, 2)), DMA((3, 2)), DMA((2,)), DMA((NX,)), DMA((HB,))]
        + [s for part in bb_parts() for s in part.scratch()] + Sums().scratch(),
        compiler_params=params(2), cost_estimate=cost(12),
    )(*args)[:2]


def adamw(w, m, v, g):
    m = 0.9 * m + 0.1 * g
    v = 0.95 * v + 0.05 * g * g
    step = m * lax.rsqrt(v + 1e-8) + 0.1 * w
    return (w - 0.02 * step).astype(BF), m, v


def solution(mesh):
    def step(x, dy, *arrays):
        weights, m, v = (arrays[i:i + 3] for i in (0, 3, 6))
        x, dy = x[0], dy[0]
        _, d0, d1, head, g0, u0, act0, h1, a1, a1T, a0T, dyT = fa(x, dy, *weights)
        gu, dn = bb(a1, a1T, dy, dyT, h1, weights[0], weights[1], head, d1.reshape(F, D), a0T, act0, g0, u0, d0.reshape(F, D))
        grads = [gu[0], gu[1], dn[:, :DR]]
        new = [adamw(w.astype(F32), m_, v_, g.astype(F32)) for w, m_, v_, g in zip(weights, m, v, grads)]
        return tuple(one[k] for k in range(3) for one in new)

    states, cut = P(("rep", "r", "s"), None, None), P(None, "s", None)
    return jax.shard_map(step, mesh=mesh, in_specs=(states, states) + (cut,) * 9, out_specs=(P("rep", "s", None),) * 9, check_vma=False)
```

time: 491 us -> 436 us (0.89)
  Pallas kernels: 470 us -> 415 us
    pallas_call x1, Pallas kernels: 353 us -> 312 us  [bb(): pl.pallas_call(bb_kernel, name='bb', out_shape=[S((PAIR, LAYERS, GR, F),...]
    pallas_call x1, Pallas kernels: 117 us -> 103 us  [fa(): pl.pallas_call(fa_kernel, name='fa', out_shape=[S((PAIR, SHARDS, GR, F),...]
where the time goes in v2:
time: 436 us; the launch traced here: 435 us
  Pallas kernels  415 us (95%)
  other arithmetic  15 us (3%)
  local copies, waits for them, and re-layouts  4.76 us (1%)
    pallas_call x1, Pallas kernels, bb(): pl.pallas_call(bb_kernel, name='bb', out_shape=[S((PAIR, LAYERS, GR, F),...  312 us
    pallas_call x1, Pallas kernels, fa(): pl.pallas_call(fa_kernel, name='fa', out_shape=[S((PAIR, SHARDS, GR, F),...  103 us
    convert_element_type x2, other arithmetic, adamw(): return ((w - 0.02 * step).astype(BF), m, v)  15 us

profile of v2, /device:TPU:2, one launch (start us, length us, event | category | flops | bytes accessed | tf_op | source)
XLA Modules:
  0.0 435.2 jit_solution(7958046169739237554)
XLA Ops:
  0.6 102.9 %fa.1 = (bf16[2,8,128,3200]{3,2,1,0:T(8,128)(2,1)}, bf16[8,400,1024]{2,1,0:T(8,128)(2,1)}, bf16[8,400,1024]{2,1,0:T(8,128)(2,1)}, bf16[2,8,128,768]{3,2,1,0:T(8,...) custom-call(bf16[2048,1024]{1,0:T(8,128)(2,1)} %bitcast.16, ...), custom_call_target="tpu_custom_call" | custom-call | flops 40265318400 | bytes 67043328 | tf_op jit(solution)/shard_map/fa/pallas_call | solution.py:828
  103.5 311.9 %bb.1 = (bf16[2,2,128,3200]{3,2,1,0:T(8,128)(2,1)}, bf16[2,512,1024]{2,1,0:T(8,128)(2,1)}, bf16[2,3200,1024]{2,1,0:T(8,128)(2,1)}, bf16[13,2048,256]{2,1,0:T(8,1...) custom-call(bf16[2048,1024]{1,0:T(8,128)(2,1)} %get-tuple-element.22.ref, ...), custom_call_target="tpu_custom_call" | custom-call | flops 161061273600 | bytes 67043328 | tf_op jit(solution)/shard_map/bb/pallas_call | solution.py:1021
  415.4 0.0 copy-start
  415.4 0.0 copy-start.1
  415.4 0.0 copy-start.2
  415.4 0.0 copy-start.3
  415.4 0.0 copy-start.4
  415.4 0.0 copy-start.5
  415.4 7.1 %fusion.8 = (bf16[2,400,1024]{2,1,0:T(8,128)(2,1)}, f32[2,400,1024]{2,1,0:T(8,128)}, f32[2,400,1024]{2,1,0:T(8,128)}) fusion(bf16[2,400,1024]{2,1,0:T(8,128)(2,1)} %refs_4_.1, bf16[2,512,1024]{2,1,0:T(8,128)(2,1)} %get-tuple-element.34, f32[2,400,1024]{2,1,0:T(8,128)} %param.21, f32[2,400,1024]{2,1,0:T(8,128)} %param.18), kind=kLoop, calls=%fused_computation.22 | loop fusion | flops 13107200 | bytes 18022400 | tf_op jit(solution)/shard_map/convert_element_type | solution.py:1037
  422.6 0.0 copy-done
  422.6 1.5 copy-done.1
  424.1 0.9 copy-done.2
  425.0 0.9 copy-done.3
  425.9 0.9 copy-done.4
  426.9 0.4 copy-done.5
  427.3 7.9 %fusion.5 = (bf16[2,128,3200]{2,1,0:T(8,128)(2,1)}, f32[2,128,3200]{2,1,0:T(8,128)}, f32[2,128,3200]{2,1,0:T(8,128)}, bf16[2,128,3200]{2,1,0:T(8,128)(2,1)}, f32...) fusion(bf16[2,128,3200]{2,1,0:T(8,128)(2,1)S(1)} %copy-done.5, bf16[2,2,128,3200]{3,2,1,0:T(8,128)(2,1)S(1)} %copy-done.4, ...), kind=kLoop, calls=%fused_computation.19 | loop fusion | flops 26214400 | bytes 36044800 | tf_op jit(solution)/shard_map/convert_element_type | solution.py:1037
Async XLA Ops:
  415.4 7.2 %copy-start = (f32[2,128,3200]{2,1,0:T(8,128)S(1)}, f32[2,128,3200]{2,1,0:T(8,128)}, u32[]{:S(2)}) copy-start(f32[2,128,3200]{2,1,0:T(8,128)} %param.20) | copy-start | bytes 9830404
  415.4 8.7 %copy-start.1 = (f32[2,128,3200]{2,1,0:T(8,128)S(1)}, f32[2,128,3200]{2,1,0:T(8,128)}, u32[]{:S(2)}) copy-start(f32[2,128,3200]{2,1,0:T(8,128)} %param.17) | copy-start | bytes 9830404
  415.4 9.6 %copy-start.2 = (f32[2,128,3200]{2,1,0:T(8,128)S(1)}, f32[2,128,3200]{2,1,0:T(8,128)}, u32[]{:S(2)}) copy-start(f32[2,128,3200]{2,1,0:T(8,128)} %param.19) | copy-start | bytes 9830404
  415.4 10.5 %copy-start.3 = (f32[2,128,3200]{2,1,0:T(8,128)S(1)}, f32[2,128,3200]{2,1,0:T(8,128)}, u32[]{:S(2)}) copy-start(f32[2,128,3200]{2,1,0:T(8,128)} %param.16) | copy-start | bytes 9830404
  415.4 11.5 %copy-start.4 = (bf16[2,2,128,3200]{3,2,1,0:T(8,128)(2,1)S(1)}, bf16[2,2,128,3200]{3,2,1,0:T(8,128)(2,1)}, u32[]{:S(2)}) copy-start(bf16[2,2,128,3200]{3,2,1,0:T(8,128)(2,1)} %get-tuple-element.33) | copy-start | bytes 9830404
  415.4 11.9 %copy-start.5 = (bf16[2,128,3200]{2,1,0:T(8,128)(2,1)S(1)}, bf16[2,128,3200]{2,1,0:T(8,128)(2,1)}, u32[]{:S(2)}) copy-start(bf16[2,128,3200]{2,1,0:T(8,128)(2,1)} %refs_6_.1) | copy-start | bytes 4915204

commit v3 on v2

--- a/solution.py
+++ b/solution.py
@@ -200,7 +200,7 @@
         sent(self.all_A() + self.O() + self.all_C() + (self.all_B() if self.route != "x" else []))
 
 
-HEAD = 3 * W
+HEAD = 4 * W
 
 
 def fa_parts():
@@ -211,10 +211,10 @@
 
 
 def bb_parts():
-    return [Gather(*a) for a in (("y", HEAD, 512), ("x", 1280, 512), ("y", 1792, 512), ("z", 2304, 896))]
-
-
-FRESH0, FRESH1 = (0, 1, 9), (3, 9)
+    return [Gather(*a) for a in (("y", HEAD, W), ("x", HEAD + W, 512), ("y", 1792, 512), ("z", 2304, 896))]
+
+
+FRESH0, FRESH1 = (0, 1), (4, 5)
 
 
 def refs_of(parts, refs):
@@ -615,10 +615,13 @@
         def step(i, _):
             for k in LATER + (1,):
                 self.gu.stage(k, *gu_item(i - OFFS[k]))
-            self.down.hook(self.dn, i)
+
+            @pl.when(i >= AT_DOWN0)
+            def _():
+                self.down.hook(self.dn, i)
             when(i, AT_DOWN1, WIDE_STEPS, lambda j: self.down.run(0, j, *beside))
             when(i, AT_DOWN1 - 1, 1, lambda _: self.down.first(0))
-            when(i, AT_DOWN0, 1, lambda _: self.down.first(1))
+            when(i, AT_DOWN0 - 1, 1, lambda _: self.down.first(1))
             when(i, AT_DOWN0, 1, after1)
             when(i, AT_TILES0 - 1, 1, before0)
             when(i, AT_DOWN0, WIDE_STEPS, lambda j: self.down.run(1, j))
@@ -641,8 +644,8 @@
     return si * u, d * u * (sg + si * (1 - sg)), d * si
 
 
-def halves(part):
-    lax.fori_loop(0, T // HALF, lambda i, _: (part(seg(i, HALF)), 0)[1], 0, unroll=True)
+def halves(part, rows=HALF):
+    lax.fori_loop(0, T // rows, lambda i, _: (part(seg(i, rows)), 0)[1], 0, unroll=True)
 
 
 def stream(n, load, store, work):
@@ -726,13 +729,15 @@
         0: [y0.pass_on, z0.pass_on, turn(0), turn(1), x0.share, x0.ready, y1.pass_on],
         1: [turn(2), y0.share, x1.share, x1.ready, y2.pass_on, y0.ready],
         2: [y1.share],
-        3: [d0y.pass_on, y1.ready],
-        4: [d1z.pass_on, d1y.pass_on, y2.share],
-        5: [turn(3), x2.share, y2.ready],
-        7: [x2.ready],
-        8: [z0.share],
-        9: [d0x.share, d0y.share, z0.ready],
-        11: [d0x.ready, d0y.ready],
+        3: [turn(3), y1.ready],
+        4: [d0y.pass_on, y2.share],
+        5: [x2.share, y2.ready],
+        6: [d1z.pass_on, d1y.pass_on],
+        7: [x2.ready, z0.share],
+        8: [z0.ready],
+        9: [d0y.share],
+        11: [d0x.share],
+        12: [d0x.ready, d0y.ready],
     }
 
     def tile(j, _):
@@ -756,7 +761,7 @@
                 start(wts(j + 1))
         done(wts(j))
 
-        @pl.when(j == LAST - 1)
+        @pl.when(j == LAST)
         def _():
             start(wds)
 
@@ -789,6 +794,9 @@
         @pl.when(i == 1)
         def _():
             d1z.share()
+
+        @pl.when(i == 3)
+        def _():
             head.share()
         t = dot(act[LAST, r, LANES:], wd[F - LANES:])
         for j in range(LAST):
@@ -887,12 +895,11 @@
     events = {
         1: [y0.pass_on, z0.pass_on],
         2: [y2.pass_on],
-        3: [y0.share, y0.ready],
-        4: [x1.share, x1.ready],
-        5: [y2.share],
+        4: [y0.share, y0.ready, x1.share],
+        5: [y2.share, x1.ready],
         6: [y2.ready],
-        8: [z0.share],
-        9: [z0.ready],
+        7: [z0.share],
+        8: [z0.ready],
     }
 
     def tile(j, _):
@@ -1010,7 +1017,7 @@
             _, dg, du = hidden(d, da[CORES * k, r], da[CORES * k + 1, r])
             dgb[0, r], dub[0, r] = dg.astype(BF), du.astype(BF)
         sums.gu.free(TILES + j, 0)
-        halves(part)
+        halves(part, GROUP)
         sums.put(TILES + j, 0, dyT[...], dgb[0])
         sums.put(TILES + j, 1, dyT[...], dub[0])
     sums.loop(tile1, (norm_loads, norm), after1, before0, tile0)

time: 436 us -> 427 us (0.979)
  Pallas kernels: 415 us -> 406 us
    pallas_call x1, Pallas kernels: 103 us -> 97.1 us  [fa(): pl.pallas_call(fa_kernel, name='fa', out_shape=[S((PAIR, SHARDS, GR, F),...]
where the time goes in v3:
time: 427 us
  Pallas kernels  406 us (95%)
  other arithmetic  15 us (4%)
  local copies, waits for them, and re-layouts  4.76 us (1%)
    pallas_call x1, Pallas kernels, bb(): pl.pallas_call(bb_kernel, name='bb', out_shape=[S((PAIR, LAYERS, GR, F),...  309 us
    pallas_call x1, Pallas kernels, fa(): pl.pallas_call(fa_kernel, name='fa', out_shape=[S((PAIR, SHARDS, GR, F),...  97.1 us
    convert_element_type x2, other arithmetic, adamw(): return ((w - 0.02 * step).astype(BF), m, v)  15 us

profile of v3, /device:TPU:2, one launch (start us, length us, event | category | flops | bytes accessed | tf_op | source)
XLA Modules:
  0.0 426.6 jit_solution(5828264441359254124)
XLA Ops:
  0.6 97.1 %fa.1 = (bf16[2,8,128,3200]{3,2,1,0:T(8,128)(2,1)}, bf16[8,400,1024]{2,1,0:T(8,128)(2,1)}, bf16[8,400,1024]{2,1,0:T(8,128)(2,1)}, bf16[2,8,128,1024]{3,2,1,0:T(8...) custom-call(bf16[2048,1024]{1,0:T(8,128)(2,1)} %bitcast.16, ...), custom_call_target="tpu_custom_call" | custom-call | flops 40265318400 | bytes 67043328 | tf_op jit(solution)/shard_map/fa/pallas_call | solution.py:836
  97.8 308.9 %bb.1 = (bf16[2,2,128,3200]{3,2,1,0:T(8,128)(2,1)}, bf16[2,512,1024]{2,1,0:T(8,128)(2,1)}, bf16[2,3200,1024]{2,1,0:T(8,128)(2,1)}, bf16[13,2048,256]{2,1,0:T(8,1...) custom-call(bf16[2048,1024]{1,0:T(8,128)(2,1)} %get-tuple-element.22.ref, ...), custom_call_target="tpu_custom_call" | custom-call | flops 161061273600 | bytes 67043328 | tf_op jit(solution)/shard_map/bb/pallas_call | solution.py:1028
  406.7 0.0 copy-start
  406.7 0.0 copy-start.1
  406.7 0.0 copy-start.2
  406.7 0.0 copy-start.3
  406.8 0.0 copy-start.4
  406.8 0.0 copy-start.5
  406.8 7.1 %fusion.8 = (bf16[2,400,1024]{2,1,0:T(8,128)(2,1)}, f32[2,400,1024]{2,1,0:T(8,128)}, f32[2,400,1024]{2,1,0:T(8,128)}) fusion(bf16[2,400,1024]{2,1,0:T(8,128)(2,1)} %refs_4_.1, bf16[2,512,1024]{2,1,0:T(8,128)(2,1)} %get-tuple-element.34, f32[2,400,1024]{2,1,0:T(8,128)} %param.21, f32[2,400,1024]{2,1,0:T(8,128)} %param.18), kind=kLoop, calls=%fused_computation.22 | loop fusion | flops 13107200 | bytes 18022400 | tf_op jit(solution)/shard_map/convert_element_type | solution.py:1044
  413.9 0.0 copy-done
  413.9 1.5 copy-done.1
  415.4 0.9 copy-done.2
  416.4 0.9 copy-done.3
  417.3 0.9 copy-done.4
  418.2 0.4 copy-done.5
  418.7 7.9 %fusion.5 = (bf16[2,128,3200]{2,1,0:T(8,128)(2,1)}, f32[2,128,3200]{2,1,0:T(8,128)}, f32[2,128,3200]{2,1,0:T(8,128)}, bf16[2,128,3200]{2,1,0:T(8,128)(2,1)}, f32...) fusion(bf16[2,128,3200]{2,1,0:T(8,128)(2,1)S(1)} %copy-done.5, bf16[2,2,128,3200]{3,2,1,0:T(8,128)(2,1)S(1)} %copy-done.4, ...), kind=kLoop, calls=%fused_computation.19 | loop fusion | flops 26214400 | bytes 36044800 | tf_op jit(solution)/shard_map/convert_element_type | solution.py:1044
Async XLA Ops:
  406.7 7.2 %copy-start = (f32[2,128,3200]{2,1,0:T(8,128)S(1)}, f32[2,128,3200]{2,1,0:T(8,128)}, u32[]{:S(2)}) copy-start(f32[2,128,3200]{2,1,0:T(8,128)} %param.20) | copy-start | bytes 9830404
  406.7 8.7 %copy-start.1 = (f32[2,128,3200]{2,1,0:T(8,128)S(1)}, f32[2,128,3200]{2,1,0:T(8,128)}, u32[]{:S(2)}) copy-start(f32[2,128,3200]{2,1,0:T(8,128)} %param.17) | copy-start | bytes 9830404
  406.7 9.6 %copy-start.2 = (f32[2,128,3200]{2,1,0:T(8,128)S(1)}, f32[2,128,3200]{2,1,0:T(8,128)}, u32[]{:S(2)}) copy-start(f32[2,128,3200]{2,1,0:T(8,128)} %param.19) | copy-start | bytes 9830404
  406.7 10.5 %copy-start.3 = (f32[2,128,3200]{2,1,0:T(8,128)S(1)}, f32[2,128,3200]{2,1,0:T(8,128)}, u32[]{:S(2)}) copy-start(f32[2,128,3200]{2,1,0:T(8,128)} %param.16) | copy-start | bytes 9830404
  406.8 11.5 %copy-start.4 = (bf16[2,2,128,3200]{3,2,1,0:T(8,128)(2,1)S(1)}, bf16[2,2,128,3200]{3,2,1,0:T(8,128)(2,1)}, u32[]{:S(2)}) copy-start(bf16[2,2,128,3200]{3,2,1,0:T(8,128)(2,1)} %get-tuple-element.33) | copy-start | bytes 9830404
  406.8 11.9 %copy-start.5 = (bf16[2,128,3200]{2,1,0:T(8,128)(2,1)S(1)}, bf16[2,128,3200]{2,1,0:T(8,128)(2,1)}, u32[]{:S(2)}) copy-start(bf16[2,128,3200]{2,1,0:T(8,128)(2,1)} %refs_6_.1) | copy-start | bytes 4915204
